TPU v7x, 128 devices: a whole 4x4x4 slice. The times are simulated.
128 devices in a mesh: blk: 32 (over y_lo, x, z), ga: 4 (over y_hi, core).
Axes of the slice: x: 4, y: 4 (y_hi: 2, y_lo: 2; y = y_hi * 2 + y_lo), z: 4, core: 2. Of those that a mesh axis runs over, the one named last changes fastest.
Arguments:
- pair_val: bfloat16 [64, 64, 16, 2048], P('blk', None, None, 'ga'), may hold values from -0.125 to 0.125
- pair_con: bfloat16 [64, 64, 16, 2048], P('blk', None, None, 'ga'), may hold values from -6 to 6
- screened: bfloat16 [64, 2048, 2048], P('blk', None, 'ga'), may hold values from -0.125 to 0.125
- amplitude: bfloat16 [64, 16], P('blk'), may hold values from -6 to 6
- qmap: int32 [64, 64], P('blk'), may hold values from 0 to 63, as said below
Outputs:
- kernel_x: float32 [64, 16], P('blk')
Inputs may be any that keep to these rules, and one draw needn't show every extreme that they name: qmap[k, k'] is the label of the difference k - k' (periodic) on a grid of 8 by 8 points, with the points and the differences labelled at random; every row and every column holds each label once.
All inputs are finite; a program needn't handle non-finite values.
Results may differ from a plain program's by a relative error of at most 0.004.
Values may be sent and summed in bfloat16 or wider, within the bound.
A program may use at most 64 MiB of HBM per device.

v0:
```python
import jax
import jax.numpy as jnp
from jax import lax
from jax.sharding import PartitionSpec as P

NV = 4
NC = 4


def in_order(tiles, dim):
    tiles = jnp.moveaxis(tiles, 0, dim)
    lengths = tiles.shape
    return tiles.reshape(*lengths[:dim], lengths[dim] * lengths[dim + 1], *lengths[dim + 2 :])


def sent_to_all(value, axis):
    devices = lax.axis_size(axis)
    return lax.all_to_all(
        jnp.broadcast_to(value[None], (devices, *value.shape)), axis, 0, 0, tiled=True
    )


def gather_directly(value, axis, dim):
    return in_order(sent_to_all(value, axis), dim)


def gathered_total(value, axis):
    return lax.all_gather(value, axis).sum(0)


def inverse_rows(qmap):
    total = qmap.shape[1]
    labels = jnp.arange(total, dtype=jnp.int32)
    hits = (qmap[:, :, None] == labels[None, None, :]).astype(jnp.int32)
    return jnp.sum(hits * labels[None, :, None], axis=1)


def kernel_unit(sent_con, screened):
    summed = jnp.einsum(
        "kqxg,qgh->kqxh",
        lax.all_gather(sent_con, "ga", axis=3, tiled=True),
        screened,
        preferred_element_type=jnp.float32,
    )
    return summed.astype(jnp.bfloat16)


def contract(unit, zeta):
    count, labels, width = (unit.shape[0], unit.shape[1], unit.shape[3])
    unit_five = unit.reshape(count, labels, NC, NC, width)
    zeta_five = zeta.reshape(count, labels, NV, NC, width)
    terms = jnp.einsum(
        "nqcyg,nqayg->nqac", unit_five, zeta_five, preferred_element_type=jnp.float32
    )
    return terms.reshape(count, labels, NV * NC)


def body(pair_val, pair_con, screened, amplitude, qmap):
    local_k, total, band_pairs, width = pair_val.shape
    every_amp = gather_directly(amplitude, "blk", 0)
    partner = inverse_rows(qmap)
    val_sorted = jnp.take_along_axis(pair_val, partner[:, :, None, None], axis=1)
    con_sorted = jnp.take_along_axis(pair_con, partner[:, :, None, None], axis=1)
    amp_sorted = every_amp[partner].reshape(local_k, total, NV, NC)
    val_five = val_sorted.reshape(local_k, total, NV, NV, width)
    zeta = jnp.einsum("kqavg,kqvc->kqacg", val_five, amp_sorted, preferred_element_type=jnp.float32)
    zeta = zeta.astype(jnp.bfloat16).reshape(local_k, total, NV * NC, width)
    sent_con = lax.all_to_all(con_sorted, "blk", split_axis=1, concat_axis=0, tiled=True)
    unit = kernel_unit(sent_con, screened)
    unit_home = lax.all_to_all(unit, "blk", split_axis=0, concat_axis=1, tiled=True)
    summed = jnp.sum(contract(unit_home, zeta), 1)
    result = gathered_total(summed, "ga")
    return result / total


def solution(mesh):
    placed = (
        P("blk", None, None, "ga"),
        P("blk", None, None, "ga"),
        P("blk", None, "ga"),
        P("blk", None),
        P("blk", None),
    )
    return jax.shard_map(
        body, mesh=mesh, in_specs=placed, out_specs=P("blk", None), check_vma=False
    )
```

profile of v0, /device:TPU:1, one launch (start us, length us, event | category | flops | bytes accessed | tf_op | source)
XLA Modules:
  0.0 187.8 jit_solution(8418440111785054035)
XLA Ops:
  6.5 0.0 all-gather.2.cloned.1.call-start
  6.5 0.9 select_reduce_fusion
  7.5 0.1 reshape.87
  7.6 0.6 copy-done
  8.1 2.2 %gather_fusion.2 = bf16[128,16,512]{2,1,0:T(8,128)(2,1)} fusion(bf16[2,64,16,512]{3,2,1,0:T(8,128)(2,1)S(1)} %copy-done, s32[128]{0:T(128)S(1)} %reshape.87), kind=kCustom, calls=%fused_computation.1.clone | custom fusion | bytes 4195328 | tf_op jit(solution)/shard_map/jit(take_along_axis)/gather | solution.py:63
  10.3 3.8 %gather_fusion.1 = bf16[128,16,512]{2,1,0:T(8,128)(2,1)} fusion(bf16[2,64,16,512]{3,2,1,0:T(8,128)(2,1)} %param.7, s32[128]{0:T(128)S(1)} %reshape.87), kind=kCustom, calls=%fused_computation.clone | custom fusion | bytes 4195328 | tf_op jit(solution)/shard_map/jit(take_along_axis)/gather | solution.py:62
  14.1 4.0 %broadcast_select_fusion.1 = (bf16[2,64,16,512]{3,2,1,0:T(8,128)(2,1)}, bf16[2,64,16,512]{3,2,1,0:T(8,128)(2,1)S(1)}) fusion(bf16[2,64,16,512]{3,2,1,0:T(8,128)(2,1)} %bitcast.55, pred[2,64]{1,0:T(4,128)(4,1)S(1)} %and_bitcast_fusion, bf16[2,64,16,512]{3,2,1,0:T(8,128)(2,1)} %bitcast.54), kind=kLoop, calls=%fused_computation.11 | loop fusion | flops 2097152 | bytes 8388736 | tf_op jit(solution)/shard_map/jit(take_along_axis)/select_n | solution.py:62
  18.1 0.2 copy.30
  18.3 36.0 %all_to_all.38 = bf16[2,64,16,512]{3,2,0,1:T(8,128)(2,1)S(1)} all-to-all(bf16[2,64,16,512]{3,2,0,1:T(8,128)(2,1)S(1)} %copy.30), channel_id=1, replica_groups=mesh['blk'=32,'ga'=4] {'blk'}, dimensions={1} | all-to-all | bytes 4194304 | tf_op jit(solution)/shard_map/all_to_all | solution.py:68
  54.3 1.6 copy.32
  55.9 0.0 all-gather.2.cloned.1.call-update
  55.9 0.6 copy-done.2
  56.5 0.6 broadcast_in_dim.8
  57.1 4.8 %all-to-all-start = ((bf16[32,2,16]{2,1,0:T(2,128)(2,1)}), bf16[32,2,16]{2,1,0:T(2,128)(2,1)S(1)}, u32[]{:S(2)}, u32[]{:S(2)}) async-start(bf16[32,2,16]{2,1,0:T(2,128)(2,1)} %broadcast_in_dim.8), calls=%async_computation | async-start | bytes 32768 | tf_op jit(solution)/shard_map/all_to_all | solution.py:18
  62.0 56.9 %all-gather.2.cloned.1.call-done = bf16[64,2,16,2048]{3,2,0,1:T(8,128)(2,1)} async-done(((bf16[64,2,16,512]{3,2,0,1:T(8,128)(2,1)}), bf16[64,2,16,2048]{3,2,0,1:T(8,128)(2,1)}) %all-gather.2.cloned.1.call-update) | async-done | bytes 8388624 | tf_op jit(solution)/shard_map/all_gather | solution.py:41
  118.9 9.1 %convert_bitcast_fusion = bf16[64,2,16,512]{3,2,0,1:T(8,128)(2,1)S(1)} fusion(bf16[64,2,16,2048]{3,2,0,1:T(8,128)(2,1)} %all-gather.2.cloned.1.call-done, bf16[2,2048,512]{2,1,0:T(8,128)(2,1)} %param.9), kind=kOutput, calls=%fused_computation.5 | convolution fusion | flops 4296015872 | bytes 14680064 | tf_op jit(solution)/shard_map/kqxg,qgh->kqxh/dot_general | solution.py:39
  128.0 1.6 copy.33
  129.6 0.0 all-to-all-done
  129.6 7.3 %all-to-all-start.2 = ((bf16[64,2,16,512]{3,2,1,0:T(8,128)(2,1)}), bf16[64,2,16,512]{3,2,1,0:T(8,128)(2,1)}, u32[]{:S(2)}, u32[]{:S(2)}) async-start(bf16[64,2,16,512]{3,2,1,0:T(8,128)(2,1)} %copy.33), calls=%async_computation.2 | async-start | bytes 4194304 | tf_op jit(solution)/shard_map/all_to_all | solution.py:70
  136.9 0.1 reshape.68
  137.0 4.0 %reshape.51 = bf16[2,64,4,4,512]{4,3,2,1,0:T(4,128)(2,1)} reshape(bf16[2,64,16,512]{3,2,1,0:T(8,128)(2,1)} %get-tuple-element.8) | data formatting | bytes 4194304 | tf_op jit(solution)/shard_map/reshape | solution.py:65
  141.0 0.7 gather_fusion
  141.7 0.1 copy.28
  141.8 0.1 reshape.50
  141.9 0.2 copy.37
  142.1 4.1 %convert_bitcast_fusion.1 = bf16[2,64,4,4,512]{4,3,2,1,0:T(4,128)(2,1)} fusion(bf16[2,64,4,4,1]{2,3,4,1,0:T(4,128)(2,1)S(1)} %copy.37, bf16[2,64,4,4,512]{4,3,2,1,0:T(4,128)(2,1)} %reshape.51), kind=kOutput, calls=%fused_computation.6 | convolution fusion | flops 9437184 | bytes 4198400 | tf_op jit(solution)/shard_map/kqavg,kqvc->kqacg/dot_general | solution.py:66
  146.2 18.3 %all-to-all-done.2 = bf16[64,2,16,512]{3,2,1,0:T(8,128)(2,1)} async-done(((bf16[64,2,16,512]{3,2,1,0:T(8,128)(2,1)}), bf16[64,2,16,512]{3,2,1,0:T(8,128)(2,1)}, u32[]{:S(2)}, u32[]{:S(2)}) %all-to-all-start.2) | async-done | bytes 2097184 | tf_op jit(solution)/shard_map/all_to_all | solution.py:70
  164.5 3.9 %copy.34 = bf16[32,2,2,16,512]{4,1,3,2,0:T(2,128)(2,1)S(1)} copy(bf16[32,2,2,16,512]{4,3,2,1,0:T(8,128)(2,1)} %bitcast.18) | data formatting | bytes 4194304 | tf_op jit(solution)/shard_map/all_to_all | solution.py:70
  168.4 3.3 %fusion.7 = f32[2,4,4]{2,1,0:T(4,128)S(1)} fusion(bf16[2,64,4,4,512]{4,0,3,2,1:T(2,128)(2,1)S(1)} %bitcast.57, bf16[2,64,4,4,512]{4,3,2,1,0:T(4,128)(2,1)S(1)} %copy-done.1), kind=kOutput, calls=%fused_computation.12 | convolution fusion | flops 8388608 | bytes 4194432 | tf_op jit(solution)/shard_map/nqcyg,nqayg->nqac/dot_general | solution.py:52
  171.7 0.1 all_gather.10
  171.8 8.6 %all_gather.11 = f32[4,2,16]{2,1,0:T(2,128)S(1)} all-gather(f32[1,2,16]{2,1,0:T(2,128)S(1)} %all_gather.10), channel_id=1, replica_groups=mesh['blk'=32,'ga'=4] {'ga'}, dimensions={0}, use_global_device_ids=true | all-gather | bytes 640 | tf_op jit(solution)/shard_map/all_gather | solution.py:28
  180.4 0.6 broadcast_multiply_fusion
  (8 shorter events, 0.0 us)
Async XLA Ops:
  6.5 1.6 copy-start
  6.5 112.4 %all-gather.2.cloned.1.call-start = ((), (), s32[]{:S(2)}) async-start(), calls=%async_computation.3 | async-start | bytes 10485760 | tf_op jit(solution)/shard_map/all_gather | solution.py:41
  55.9 0.7 copy-start.2
  57.1 72.5 %all-to-all-start = ((bf16[32,2,16]{2,1,0:T(2,128)(2,1)}), bf16[32,2,16]{2,1,0:T(2,128)(2,1)S(1)}, u32[]{:S(2)}, u32[]{:S(2)}) async-start(bf16[32,2,16]{2,1,0:T(2,128)(2,1)} %broadcast_in_dim.8), calls=%async_computation | async-start | bytes 32768 | tf_op jit(solution)/shard_map/all_to_all | solution.py:18
  129.6 34.9 %all-to-all-start.2 = ((bf16[64,2,16,512]{3,2,1,0:T(8,128)(2,1)}), bf16[64,2,16,512]{3,2,1,0:T(8,128)(2,1)}, u32[]{:S(2)}, u32[]{:S(2)}) async-start(bf16[64,2,16,512]{3,2,1,0:T(8,128)(2,1)} %copy.33), calls=%async_computation.2 | async-start | bytes 4194304 | tf_op jit(solution)/shard_map/all_to_all | solution.py:70
  164.5 3.9 %copy-start.1 = (bf16[2,64,4,4,512]{4,3,2,1,0:T(4,128)(2,1)S(1)}, bf16[2,64,4,4,512]{4,3,2,1,0:T(4,128)(2,1)}, u32[]{:S(2)}) copy-start(bf16[2,64,4,4,512]{4,3,2,1,0:T(4,128)(2,1)} %convert_bitcast_fusion.1) | copy-start | bytes 6291460
Sparse Core Ops, SparseCore 0:
  56.0 62.8 all-gather.1
where the time goes:
time: 188 us
  waiting for transfers between devices  75.2 us (40%)
  blocking collectives  44.5 us (24%)
  local copies, waits for them, and re-layouts  20.4 us (11%)
  matrix products  16.5 us (9%)
  between operations  13.5 us (7%)
  starting transfers between devices  12.1 us (6%)
  other arithmetic  5.55 us (3%)
    all_gather x1, waiting for transfers between devices, kernel_unit(): lax.all_gather(sent_con, 'ga', axis=3, tiled=True)  56.9 us
    all_to_all x1, blocking collectives, body(): lax.all_to_all(con_sorted, 'blk', split_axis=1, concat_axis=0, tiled=True)  36 us
    all_to_all x1, waiting for transfers between devices, body(): lax.all_to_all(unit, 'blk', split_axis=0, concat_axis=1, tiled=True)  18.3 us
    dot_general x1, matrix products, kernel_unit(): jnp.einsum('kqxg,qgh->kqxh', lax.all_gather(sent_con, 'ga', axis=3, tiled...  9.05 us
    all_gather x1, blocking collectives, gathered_total(): return lax.all_gather(value, axis).sum(0)  8.57 us
    all_to_all x1, starting transfers between devices, body(): lax.all_to_all(unit, 'blk', split_axis=0, concat_axis=1, tiled=True)  7.28 us
    all_to_all x1, starting transfers between devices, sent_to_all(): lax.all_to_all(jnp.broadcast_to(value[None], (devices, *value.shape)), ax...  4.85 us
    dot_general x1, matrix products, body(): jnp.einsum('kqavg,kqvc->kqacg', val_five, amp_sorted, preferred_element_t...  4.14 us
  transfers between devices with their start and end apart: 3, of which 2 were waited for; matrix products, arithmetic and copies ran while one was open for 11% of the time, Pallas kernels for 0%

commit v1 on v0

v1 whole, which is shorter than its diff:
```python
import functools

import jax
import jax.numpy as jnp
from jax import lax
from jax.experimental import pallas as pl
from jax.experimental.pallas import tpu as pltpu
from jax.sharding import PartitionSpec as P

MESH = pl.DeviceIdType.MESH
ORDER = ((0, 0), (1, 0), (3, 0), (0, 1), (0, 3), (1, 1), (3, 3), (1, 3), (3, 1), (2, 0), (0, 2), (2, 1), (1, 2), (2, 3), (3, 2), (2, 2))
LAG = 2


def inverse_rows(qmap):
    total = qmap.shape[1]
    labels = jnp.arange(total, dtype=jnp.int32)
    hits = (qmap[:, :, None] == labels[None, None, :]).astype(jnp.int32)
    return jnp.sum(hits * labels[None, :, None], axis=1)


def iota(shape, dim):
    return lax.broadcasted_iota(jnp.int32, shape, dim)


def zero_one(cond):
    return jnp.where(cond, 1.0, 0.0).astype(jnp.bfloat16)


def kernel(
    partner, con_hbm, val_hbm, w_hbm, qa_ref, out_ref,
    con_raw, val_raw, w, s_send, d_send, val_send, con_all, val_all, transit,
    unit, acc, weight, qa_all, part, res, fin,
    load_sem, s_rs, d_rs, y_rs, p_rs, val_rs, qa_rs, res_rs, fin_rs,
    con_ss, val_ss, relay_ss, d2d_ss, qa_ss, res_ss, fin_ss,
):
    blk, ga = lax.axis_index("blk"), lax.axis_index("ga")
    lo, x, z = blk // 16, (blk // 4) % 4, blk % 4
    h, c = ga // 2, ga % 2

    def dev(dx, dz, flip_lo=0, flip_h=0, flip_c=0):
        to_lo = (lo + flip_lo) % 2
        to_h = (h + flip_h) % 2
        to_c = (c + flip_c) % 2
        return (to_lo * 16 + ((x + dx + 4) % 4) * 4 + (z + dz + 4) % 4, to_h * 2 + to_c)

    barrier = pltpu.get_barrier_semaphore()
    greeted = [dev(-dx, -dz, fl) for dx, dz in ORDER for fl in (0, 1) if (dx, dz, fl) != (0, 0, 0)]
    greeted += [dev(0, 0, 0, 1), dev(0, 0, 1, 1), dev(0, 0, 0, 0, 1), dev(0, 0, 0, 1, 1)]
    for other in greeted:
        pl.semaphore_signal(barrier, inc=1, device_id=other, device_id_type=MESH)

    loads = [
        pltpu.make_async_copy(con_hbm, con_raw, load_sem.at[0]),
        pltpu.make_async_copy(val_hbm, val_raw, load_sem.at[1]),
        pltpu.make_async_copy(w_hbm, w, load_sem.at[2]),
    ]
    for load in loads:
        load.start()

    def send(src, dst, ss, rs, to):
        copy = pltpu.make_async_remote_copy(src, dst, ss, rs, device_id=to, device_id_type=MESH)
        copy.start()
        return copy

    def arrived(dst, rs):
        pltpu.make_async_copy(dst, dst, rs).wait()

    def labels_of(dx, dz, fl):
        to, _ = dev(dx, dz, fl)
        return to * 2

    qa_all[blk] = qa_ref[...]
    loads[0].wait()
    for t, (dx, dz) in enumerate(ORDER):
        for fl in (0, 1):
            first = labels_of(dx, dz, fl)
            for q in (0, 1):
                for k in (0, 1):
                    tile = con_raw[k, partner[k, first + q]]
                    if fl == 0 and t == 0:
                        con_all[0, 0, 0, 0, q, k] = tile
                    elif fl == 0:
                        s_send[t, q, k] = tile
                    elif t == 0:
                        transit[0, q, k] = tile
                    else:
                        d_send[t, q, k] = tile
    pl.semaphore_wait(barrier, len(greeted))

    for t, (dx, dz) in enumerate(ORDER):
        if t:
            to = dev(dx, dz)
            send(d_send.at[t], transit.at[t], con_ss.at[0], d_rs.at[t], to)
            send(s_send.at[t], con_all.at[0, 0, t, 0], con_ss.at[1], s_rs.at[t], to)

    def relay(t):
        if t:
            arrived(transit.at[t], d_rs.at[t])
        send(transit.at[t], con_all.at[0, 0, t, 1], relay_ss.at[0], y_rs.at[0, t], dev(0, 0, 1))
        send(transit.at[t], con_all.at[0, 1, t, 1], relay_ss.at[1], y_rs.at[1, t], dev(0, 0, 1, 1))
        here = con_all.at[0, 0, t, 0]
        if t:
            arrived(here, s_rs.at[t])
        send(here, con_all.at[0, 1, t, 0], relay_ss.at[2], y_rs.at[2, t], dev(0, 0, 0, 1))
        send(here, con_all.at[1, 0, t, 0], d2d_ss.at[3], p_rs.at[3, t], dev(0, 0, 0, 0, 1))

    COLUMN = ((0, 1), (1, 1), (1, 0))

    def forward(t):
        for n, (gh, fl) in enumerate(COLUMN):
            arrived(con_all.at[0, gh, t, fl], y_rs.at[n, t])
            send(con_all.at[0, gh, t, fl], con_all.at[1, gh, t, fl], d2d_ss.at[n], p_rs.at[n, t], dev(0, 0, 0, 0, 1))

    relay(0)

    loads[1].wait()
    for t, (dx, dz) in enumerate(ORDER):
        for fl in (0, 1):
            first = labels_of(dx, dz, fl)
            for q in (0, 1):
                for k in (0, 1):
                    tile = val_raw[k, partner[k, first + q]]
                    if fl == 0 and t == 0:
                        val_all[0, q, k] = tile
                    else:
                        val_send[t * 2 + fl, q, k] = tile

    for t, (dx, dz) in enumerate(ORDER):
        for fl in (0, 1):
            if t or fl:
                send(qa_ref, qa_all.at[blk], qa_ss, qa_rs, dev(dx, dz, fl))
    for t, (dx, dz) in enumerate(ORDER):
        for fl in (1, 0):
            if t or fl:
                send(val_send.at[t * 2 + fl], val_all.at[t * 2 + fl], val_ss, val_rs.at[t * 2 + fl], dev(dx, dz, fl))

    def weights():
        arrived(qa_all.at[pl.ds(1, 31)], qa_rs)
        every = qa_all[...].reshape(64, 128)
        amps = every.astype(jnp.bfloat16)
        pick = zero_one(iota((128, 128), 0) == iota((128, 128), 1) + 64)
        amps = jnp.dot(amps, pick, preferred_element_type=jnp.float32).astype(jnp.bfloat16)
        row = iota((64, 64), 0)
        source = jnp.zeros((64, 64), jnp.int32)
        for t, (dx, dz) in enumerate(ORDER):
            for fl in (0, 1):
                source = jnp.where(row // 2 == t * 2 + fl, labels_of(-dx, -dz, fl), source)
        perm = zero_one(source + row % 2 == iota((64, 64), 1))
        for q in (0, 1):
            mine = (blk * 2 + q).astype(jnp.float32)
            hot = zero_one(every[:, :64] == mine)
            chosen = jnp.dot(hot, amps, preferred_element_type=jnp.float32).astype(jnp.bfloat16)
            chosen = jnp.dot(perm, chosen, preferred_element_type=jnp.float32).astype(jnp.bfloat16)
            spread = zero_one(iota((256, 16), 0) // 16 == iota((256, 16), 1))
            columns = zero_one((iota((128, 256), 0) // 4 == iota((128, 256), 1) % 4) & (iota((128, 256), 0) < 16))
            for a in range(4):
                rows = jnp.dot(spread, chosen[16 * a : 16 * a + 16], preferred_element_type=jnp.float32)
                rows = jnp.where(iota((256, 128), 0) % 4 == iota((256, 128), 1) % 4, rows, 0.0).astype(jnp.bfloat16)
                full = jnp.dot(rows, columns, preferred_element_type=jnp.float32)
                same = iota((256, 256), 0) // 16 == iota((256, 256), 1) // 16
                weight[q, a] = jnp.where(same, full, 0.0).astype(jnp.bfloat16)

    def units(a):
        for t in range(4 * a, 4 * a + 4):
            for n, (gh, fl) in enumerate(COLUMN + ((0, 0),)):
                arrived(con_all.at[1, gh, t, fl], p_rs.at[n, t])
        for q in (0, 1):

            def quarter(n, carry):
                gc, gh = n // 2, n % 2
                g = ((h + gh) % 2) * 2 + (c + gc) % 2
                lhs = con_all[gc, gh, 4 * a : 4 * a + 4, :, q].reshape(256, 512)
                rhs = w[q, pl.ds(pl.multiple_of(g * 512, 512), 512), :]
                acc[...] += jnp.dot(lhs, rhs, preferred_element_type=jnp.float32)
                return carry

            acc[...] = jnp.zeros_like(acc)
            lax.fori_loop(0, 4, quarter, 0)
            unit[q, a] = acc[...].astype(jnp.bfloat16)

    def terms(a):
        for t in range(4 * a, 4 * a + 4):
            for fl in (0, 1):
                if t or fl:
                    arrived(val_all.at[t * 2 + fl], val_rs.at[t * 2 + fl])
        total = jnp.zeros((256, 256), jnp.float32)
        for q in (0, 1):
            vals = val_all[8 * a : 8 * a + 8, q].reshape(256, 512)
            full = lax.dot_general(unit[q, a], vals, (((1,), (1,)), ((), ())), preferred_element_type=jnp.float32)
            total = total + full * weight[q, a].astype(jnp.float32)
        lanes = iota((256, 128), 1)
        columns = jnp.where(((iota((256, 128), 0) // 4) % 4 == lanes // 4) & (lanes < 16), 1.0, 0.0)
        summed = jnp.dot(total, columns, preferred_element_type=jnp.float32, precision=lax.Precision.HIGHEST)
        summed = jnp.where((iota((256, 128), 0) // 4) % 4 == lanes % 4, summed, 0.0)
        part[4 * a : 4 * a + 4] = jnp.sum(summed.reshape(16, 16, 128), axis=1).reshape(4, 2, 2, 128)

    for step in range(1, 16):
        relay(step)
        if step >= LAG:
            forward(step - LAG)
        if step == 3:
            loads[2].wait()
            weights()
        done = step - LAG - 1
        if done >= 3 and done % 4 == 3:
            units(done // 4)
    for t in range(16 - LAG, 16):
        forward(t)
    units(3)
    for a in range(4):
        terms(a)

    res[0] = part[0, 0]
    for t, (dx, dz) in enumerate(ORDER):
        for fl in (0, 1):
            if t or fl:
                send(part.at[t, fl], res.at[t * 2 + fl], res_ss, res_rs, dev(-dx, -dz, fl))
    arrived(res.at[pl.ds(1, 31)], res_rs)
    fin[ga] = jnp.sum(res[...], axis=0)
    for n, (gh, gc) in enumerate(((0, 1), (1, 0), (1, 1))):
        send(fin.at[ga], fin.at[ga], fin_ss.at[n], fin_rs, dev(0, 0, 0, gh, gc))
    arrived(fin.at[pl.ds(1, 3)], fin_rs)
    total = jnp.sum(fin[...], axis=0)
    out_ref[...] = total[:, :16] / 64.0

    def sent(src, ss):
        pltpu.make_async_copy(src, src, ss).wait()

    sent(d_send.at[pl.ds(1, 15)], con_ss.at[0])
    sent(s_send.at[pl.ds(1, 15)], con_ss.at[1])
    for n in range(3):
        sent(transit, relay_ss.at[n])
    for n in range(4):
        sent(transit, d2d_ss.at[n])
    sent(val_send.at[pl.ds(1, 31)], val_ss)
    sent(qa_all.at[pl.ds(1, 31)], qa_ss)
    sent(res.at[pl.ds(1, 31)], res_ss)
    for n in range(3):
        sent(fin.at[0], fin_ss.at[n])


def body(pair_val, pair_con, screened, amplitude, qmap):
    partner = inverse_rows(qmap)
    qa = jnp.concatenate(
        [qmap.astype(jnp.float32), amplitude.astype(jnp.float32), jnp.zeros((2, 48), jnp.float32)], axis=1
    )
    bf16, f32 = jnp.bfloat16, jnp.float32
    block = (2, 2, 16, 512)
    dma = pltpu.SemaphoreType.DMA
    any_space = pl.BlockSpec(memory_space=pl.ANY)
    vmem = pl.BlockSpec(memory_space=pltpu.VMEM)
    return pl.pallas_call(
        kernel,
        out_shape=jax.ShapeDtypeStruct((2, 16), f32),
        in_specs=[pl.BlockSpec(memory_space=pltpu.SMEM), any_space, any_space, any_space, vmem],
        out_specs=vmem,
        scratch_shapes=[
            pltpu.VMEM((2, 64, 16, 512), bf16),
            pltpu.VMEM((2, 64, 16, 512), bf16),
            pltpu.VMEM((2, 2048, 512), bf16),
            pltpu.VMEM((16, *block), bf16),
            pltpu.VMEM((16, *block), bf16),
            pltpu.VMEM((32, *block), bf16),
            pltpu.VMEM((2, 2, 16, 2, *block), bf16),
            pltpu.VMEM((32, *block), bf16),
            pltpu.VMEM((16, *block), bf16),
            pltpu.VMEM((2, 4, 256, 512), bf16),
            pltpu.VMEM((256, 512), f32),
            pltpu.VMEM((2, 4, 256, 256), bf16),
            pltpu.VMEM((32, 2, 128), f32),
            pltpu.VMEM((16, 2, 2, 128), f32),
            pltpu.VMEM((32, 2, 128), f32),
            pltpu.VMEM((4, 2, 128), f32),
            dma((3,)), dma((16,)), dma((16,)), dma((3, 16)), dma((4, 16)), dma((32,)), dma, dma, dma,
            dma((2,)), dma, dma((3,)), dma((4,)), dma, dma, dma((3,)),
        ],
        compiler_params=pltpu.CompilerParams(collective_id=0, has_side_effects=True),
    )(partner, pair_con, pair_val, screened, qa)


def solution(mesh):
    placed = (
        P("blk", None, None, "ga"),
        P("blk", None, None, "ga"),
        P("blk", None, "ga"),
        P("blk", None),
        P("blk", None),
    )
    return jax.shard_map(
        body, mesh=mesh, in_specs=placed, out_specs=P("blk", None), check_vma=False
    )
```

time: 188 us -> 110 us (0.59)
  Pallas kernels: 0 us -> 106 us
  waiting for transfers between devices: 75.2 us -> 0 us
  blocking collectives: 44.5 us -> 0 us
  local copies, waits for them, and re-layouts: 20.4 us -> 1.3 us
  matrix products: 16.5 us -> 0 us
  between operations: 13.5 us -> 0.01 us
  starting transfers between devices: 12.1 us -> 0 us
  other arithmetic: 5.55 us -> 3.34 us
    pallas_call x0 -> x1, Pallas kernels: none -> 106 us  [body(): pl.pallas_call(kernel, out_shape=jax.ShapeDtypeStruct((2, 16), f32), in_s...]
    all_gather x1 -> x0, waiting for transfers between devices: 56.9 us -> none  [kernel_unit(): lax.all_gather(sent_con, 'ga', axis=3, tiled=True)]
    all_to_all x1 -> x0, blocking collectives: 36 us -> none  [body(): lax.all_to_all(con_sorted, 'blk', split_axis=1, concat_axis=0, tiled=True)]
    all_to_all x2 -> x0, waiting for transfers between devices: 18.3 us -> none  [the longest x1 18.3 us: body(): lax.all_to_all(unit, 'blk', split_axis=0, concat_axis=1, tiled=True)]
    dot_general x3 -> x0, matrix products: 16.5 us -> none  [the longest x1 9.05 us: kernel_unit(): jnp.einsum('kqxg,qgh->kqxh', lax.all_gather(sent_con, 'ga', axis=3, tiled...]
    all_to_all x2 -> x0, starting transfers between devices: 12.1 us -> none  [the longest x1 7.28 us: body(): lax.all_to_all(unit, 'blk', split_axis=0, concat_axis=1, tiled=True)]
    all_gather x1 -> x0, blocking collectives: 8.57 us -> none  [gathered_total(): return lax.all_gather(value, axis).sum(0)]
    gather x5 -> x0, local copies, waits for them, and re-layouts: 6.83 us -> none  [the longest x2 3.88 us: body(): jnp.take_along_axis(pair_val, partner[:, :, None, None], axis=1)]
  transfers between devices with their start and end apart: 3 -> 0, of which waited for: 2 -> 0; matrix products, arithmetic and copies ran while one was open for 11% -> 0% of each run, Pallas kernels for 0% -> 0%
where the time goes in v1:
time: 110 us
  Pallas kernels  106 us (96%)
  other arithmetic  3.34 us (3%)
  local copies, waits for them, and re-layouts  1.3 us (1%)
    pallas_call x1, Pallas kernels, body(): pl.pallas_call(kernel, out_shape=jax.ShapeDtypeStruct((2, 16), f32), in_s...  106 us

profile of v1, /device:TPU:1, one launch (start us, length us, event | category | flops | bytes accessed | tf_op | source)
XLA Modules:
  0.0 110.2 jit_solution(2308970476012651600)
XLA Ops:
  0.0 0.1 pad.2.clone
  0.1 0.7 convert_element_type.8
  0.7 0.7 convert_element_type.7
  1.4 0.7 maximum_maximum_fusion.qa_ref
  2.1 1.3 %select_reduce_fusion.partner = s32[2,64]{1,0:T(2,128)} fusion(s32[2,64]{1,0:T(2,128)} %param.9), kind=kLoop, calls=%fused_computation | loop fusion | flops 24448 | bytes 1024 | tf_op jit(solution)/shard_map/reduce_sum | solution.py:19
  3.4 105.6 %shard_map.55 = f32[2,16]{1,0:T(2,128)} custom-call(s32[2,64]{1,0:T(2,128)} %select_reduce_fusion.partner, bf16[2,64,16,512]{3,2,1,0:T(8,128)(2,1)} %con_hbm.1, bf16[2,64,16,512]{3,2,1,0:T(8,128)(2,1)} %val_hbm.1, bf16[2,2048,512]{2,1,0:T(8,128)(2,1)} %w_hbm.1, f32[2,128]{1,0:T(2,128)} %maximum_maximum_fusion.qa_ref), custom_call_target="tpu_custom_call" | custom-call | tf_op jit(solution)/shard_map/pallas_call | solution.py:253
  109.0 1.2 %copy.7 = f32[2,16]{1,0:T(2,128)} copy(f32[2,16]{1,0:T(2,128)} %shard_map.55) | data formatting | bytes 256
  (1 shorter events, 0.0 us)

commit v2 on v1

v2 whole, which is shorter than its diff:
```python
import jax
import jax.numpy as jnp
from jax import lax
from jax.experimental import pallas as pl
from jax.experimental.pallas import tpu as pltpu
from jax.sharding import PartitionSpec as P

MESH = pl.DeviceIdType.MESH
ORDER = ((2, 2), (1, 1), (3, 3), (1, 3), (3, 1), (2, 1), (1, 2), (2, 3), (3, 2), (2, 0), (0, 2), (0, 3), (1, 0), (3, 0), (0, 1), (0, 0))
HERE = 15
GROUPS = ((0, 4), (4, 4), (8, 4), (12, 3), (15, 1))
QUARTERS = ((0, 0), (0, 1), (1, 0), (1, 1))
COLUMN = ((0, 1), (1, 1), (1, 0))


def iota(shape, dim):
    return lax.broadcasted_iota(jnp.int32, shape, dim)


def zero_one(cond):
    return jnp.where(cond, 1.0, 0.0).astype(jnp.bfloat16)


def hops(offset):
    dx, dz, fl, gh, _ = offset
    return min(dx, 4 - dx) + min(dz, 4 - dz) + (2 if gh and not fl else fl)


def kernel(
    con_hbm, val_hbm, w_hbm, amp_ref, qmap_ref, out_ref,
    con_raw, val_raw, w, s_send, d_send, vs_send, vd_send, con_all, val_all, transit, val_transit,
    acc, weight, rows_ref, partner, qa_all, part, res, fin, last,
    load_sem, s_rs, d_rs, y_rs, p_rs, val_rs, vt_rs, qa_rs, res_rs, fin_rs, last_rs,
    con_ss, val_ss, relay_ss, d2d_ss, qa_ss, res_ss, fin_ss, last_ss,
):
    blk, ga = lax.axis_index("blk"), lax.axis_index("ga")
    lo, x, z = blk // 16, (blk // 4) % 4, blk % 4
    h, c = ga // 2, ga % 2

    def dev(dx, dz, flip_lo=0, flip_h=0, flip_c=0):
        to_lo = (lo + flip_lo) % 2
        to_h = (h + flip_h) % 2
        to_c = (c + flip_c) % 2
        return (to_lo * 16 + ((x + dx + 4) % 4) * 4 + (z + dz + 4) % 4, to_h * 2 + to_c)

    loads = [
        pltpu.make_async_copy(con_hbm, con_raw, load_sem.at[0]),
        pltpu.make_async_copy(val_hbm, val_raw, load_sem.at[1]),
        pltpu.make_async_copy(w_hbm, w, load_sem.at[2]),
    ]
    for load in loads:
        load.start()

    peers = {(dx, dz, fl, 0, 0) for dx, dz in ORDER for fl in (0, 1)}
    peers |= {((4 - dx) % 4, (4 - dz) % 4, fl, gh, gc) for dx, dz in ORDER[12:] for fl in (0, 1) for gh in (0, 1) for gc in (0, 1)}
    peers |= {(dx, dz, fl, gh, gc) for dx, dz in ORDER[12:] for fl in (0, 1) for gh in (0, 1) for gc in (0, 1)}
    peers = sorted(peers - {(0, 0, 0, 0, 0)}, key=lambda p: (-hops(p), p))
    barrier = pltpu.get_barrier_semaphore()
    for offset in peers:
        pl.semaphore_signal(barrier, inc=1, device_id=dev(*offset), device_id_type=MESH)

    def send(src, dst, ss, rs, to):
        pltpu.make_async_remote_copy(src, dst, ss, rs, device_id=to, device_id_type=MESH).start()

    def arrived(dst, rs):
        pltpu.make_async_copy(dst, dst, rs).wait()

    sent = arrived

    qmap = qmap_ref[...]
    for k in (0, 1):
        hit = qmap[k : k + 1, :] == iota((64, 64), 0)
        column = jnp.max(jnp.where(hit, iota((64, 64), 1), 0), axis=1, keepdims=True)
        square = jnp.where(iota((64, 64), 0) == iota((64, 64), 1), column, 0)
        rows_ref[k : k + 1, :] = jnp.max(square, axis=0, keepdims=True)
    to_smem = pltpu.make_async_copy(rows_ref, partner, load_sem.at[3])
    to_smem.start()
    place = zero_one(iota((16, 128), 0) + 64 == iota((16, 128), 1))
    moved = jnp.dot(amp_ref[...], place, preferred_element_type=jnp.float32)
    qa_all[blk] = moved + jnp.concatenate([qmap.astype(jnp.float32), jnp.zeros((2, 64), jnp.float32)], axis=1)
    to_smem.wait()

    loads[0].wait()
    for t, (dx, dz) in enumerate(ORDER):
        for fl, buffer in ((1, d_send), (0, s_send)):
            first = dev(dx, dz, fl)[0] * 2
            for q in (0, 1):
                for k in (0, 1):
                    tile = con_raw[k, partner[k, first + q]]
                    if t != HERE:
                        buffer[t, q, k] = tile
                    elif fl:
                        transit[HERE, q, k] = tile
                    else:
                        con_all[0, 0, HERE, 0, q, k] = tile
    loads[1].wait()
    for t, (dx, dz) in enumerate(ORDER):
        for fl, buffer in ((1, vd_send), (0, vs_send)):
            first = dev(dx, dz, fl)[0] * 2
            for q in (0, 1):
                for k in (0, 1):
                    tile = val_raw[k, partner[k, first + q]]
                    if t == HERE and not fl:
                        val_all[2 * HERE, q, k] = tile
                    else:
                        buffer[t, q, k] = tile
    pl.semaphore_wait(barrier, len(peers))

    def val_along_y(t):
        if t == HERE:
            send(vd_send.at[t], val_all.at[2 * t + 1], val_ss.at[1], val_rs.at[2 * t + 1], dev(0, 0, 1))
        else:
            send(vd_send.at[t], val_transit.at[t], val_ss.at[1], vt_rs.at[t], dev(0, 0, 1))

    def val_onward(t):
        arrived(val_transit.at[t], vt_rs.at[t])
        send(val_transit.at[t], val_all.at[2 * t + 1], val_ss.at[2], val_rs.at[2 * t + 1], dev(*ORDER[t]))

    for t in range(16):
        val_along_y(t)
    for block in range(0, 15, 4):
        for t in range(block, min(block + 4, 15)):
            send(d_send.at[t], transit.at[t], con_ss.at[0], d_rs.at[t], dev(*ORDER[t]))
        for t in range(block, min(block + 4, 15)):
            send(s_send.at[t], con_all.at[0, 0, t, 0], con_ss.at[1], s_rs.at[t], dev(*ORDER[t]))
    for t in range(15):
        send(vs_send.at[t], val_all.at[2 * t], val_ss.at[0], val_rs.at[2 * t], dev(*ORDER[t]))
    for t, (dx, dz) in enumerate(ORDER):
        for fl in (0, 1):
            if t != HERE or fl:
                send(qa_all.at[blk], qa_all.at[blk], qa_ss, qa_rs, dev(dx, dz, fl))

    def relay(t):
        if t != HERE:
            arrived(transit.at[t], d_rs.at[t])
        send(transit.at[t], con_all.at[0, 0, t, 1], relay_ss.at[0], y_rs.at[0, t], dev(0, 0, 1))
        send(transit.at[t], con_all.at[0, 1, t, 1], relay_ss.at[1], y_rs.at[1, t], dev(0, 0, 1, 1))
        here = con_all.at[0, 0, t, 0]
        if t != HERE:
            arrived(here, s_rs.at[t])
        send(here, con_all.at[0, 1, t, 0], relay_ss.at[2], y_rs.at[2, t], dev(0, 0, 0, 1))
        send(here, con_all.at[1, 0, t, 0], d2d_ss.at[3], p_rs.at[3, t], dev(0, 0, 0, 0, 1))

    def forward(t, n):
        gh, fl = COLUMN[n]
        arrived(con_all.at[0, gh, t, fl], y_rs.at[n, t])
        send(con_all.at[0, gh, t, fl], con_all.at[1, gh, t, fl], d2d_ss.at[n], p_rs.at[n, t], dev(0, 0, 0, 0, 1))

    def weights():
        arrived(qa_all.at[pl.ds(1, 31)], qa_rs)
        every = qa_all[...].reshape(64, 128)
        amps = every.astype(jnp.bfloat16)
        pick = zero_one(iota((128, 128), 0) == iota((128, 128), 1) + 64)
        amps = jnp.dot(amps, pick, preferred_element_type=jnp.float32).astype(jnp.bfloat16)
        row = iota((64, 64), 0)
        source = jnp.zeros((64, 64), jnp.int32)
        for t, (dx, dz) in enumerate(ORDER):
            for fl in (0, 1):
                source = jnp.where(row // 2 == t * 2 + fl, dev(-dx, -dz, fl)[0] * 2, source)
        perm = zero_one(source + row % 2 == iota((64, 64), 1))
        for q in (0, 1):
            mine = (blk * 2 + q).astype(jnp.float32)
            hot = zero_one(every[:, :64] == mine)
            chosen = jnp.dot(hot, amps, preferred_element_type=jnp.float32).astype(jnp.bfloat16)
            chosen = jnp.dot(perm, chosen, preferred_element_type=jnp.float32).astype(jnp.bfloat16)
            spread = zero_one(iota((256, 16), 0) // 16 == iota((256, 16), 1))
            columns = zero_one((iota((128, 256), 0) // 4 == iota((128, 256), 1) % 4) & (iota((128, 256), 0) < 16))
            for t0, n in GROUPS:
                rows = jnp.dot(spread[: 64 * n, : 4 * n], chosen[4 * t0 : 4 * (t0 + n)], preferred_element_type=jnp.float32)
                rows = jnp.where(iota((64 * n, 128), 0) % 4 == iota((64 * n, 128), 1) % 4, rows, 0.0).astype(jnp.bfloat16)
                full = jnp.dot(rows, columns, preferred_element_type=jnp.float32)
                same = iota((64 * n, 256), 0) // 16 == iota((64 * n, 256), 1) // 16
                weight[q, 64 * t0 : 64 * (t0 + n)] = jnp.where(same, full, 0.0).astype(jnp.bfloat16)

    def from_partner(t0, n, gh):
        for t in range(t0, t0 + n):
            for m, (of_h, fl) in enumerate(COLUMN + ((0, 0),)):
                if of_h == gh:
                    arrived(con_all.at[1, gh, t, fl], p_rs.at[m, t])

    def quarter(t0, n, gc, gh, first=False):
        g = ((h + gh) % 2) * 2 + (c + gc) % 2

        def one(q, carry):
            lhs = con_all[gc, gh, t0 : t0 + n, :, q].reshape(64 * n, 512)
            rhs = w[q, pl.ds(pl.multiple_of(g * 512, 512), 512), :]
            product = jnp.dot(lhs, rhs, preferred_element_type=jnp.float32)
            if first:
                acc[q, : 64 * n] = product
            else:
                acc[q, : 64 * n] += product
            return carry

        lax.fori_loop(0, 2, one, 0)

    def units(t0, n):
        for gc, gh in QUARTERS:
            if gc:
                from_partner(t0, n, gh)
            quarter(t0, n, gc, gh, first=(gc, gh) == (0, 0))

    def terms(t0, n):
        for t in range(t0, t0 + n):
            for fl in (0, 1):
                if t != HERE or fl:
                    arrived(val_all.at[t * 2 + fl], val_rs.at[t * 2 + fl])
        size = 64 * n
        total = jnp.zeros((size, size), jnp.float32)
        for q in (0, 1):
            vals = val_all[2 * t0 : 2 * (t0 + n), q].reshape(size, 512)
            unit = acc[q, :size].astype(jnp.bfloat16)
            full = lax.dot_general(unit, vals, (((1,), (1,)), ((), ())), preferred_element_type=jnp.float32)
            total = total + full * weight[q, 64 * t0 : 64 * (t0 + n), :size].astype(jnp.float32)
        lanes = iota((size, 128), 1)
        columns = jnp.where(((iota((size, 128), 0) // 4) % 4 == lanes // 4) & (lanes < 16), 1.0, 0.0)
        summed = jnp.dot(total, columns, preferred_element_type=jnp.float32, precision=lax.Precision.HIGHEST)
        summed = jnp.where((iota((size, 128), 0) // 4) % 4 == lanes % 4, summed, 0.0)
        part[2 * t0 : 2 * (t0 + n)] = jnp.sum(summed.reshape(4 * n, 16, 128), axis=1).reshape(2 * n, 2, 128)

    def home(t0, n, ss, rs):
        for t in range(t0, t0 + n):
            dx, dz = ORDER[t]
            for fl in (0, 1):
                for gh in (0, 1):
                    for gc in (0, 1):
                        if (dx, dz, fl, gh, gc) != (0, 0, 0, 0, 0):
                            slot = ((t - 12) * 2 + fl) * 4 + ga
                            send(part.at[t * 2 + fl], last.at[slot], ss, rs, dev(-dx, -dz, fl, gh, gc))

    for t in range(16):
        relay(t)
        if t != HERE:
            val_onward(t)
    weights()
    loads[2].wait()
    for t in range(15):
        for n in range(3):
            forward(t, n)
        if t in (5, 9, 13):
            units(t - 5, 4)
            terms(t - 5, 4)
        if t == 13:
            for u, (dx, dz) in enumerate(ORDER[:12]):
                for fl in (0, 1):
                    send(part.at[u * 2 + fl], res.at[u * 2 + fl], res_ss, res_rs, dev(-dx, -dz, fl))
    units(12, 3)
    terms(12, 3)
    home(12, 3, last_ss.at[0], last_rs.at[0])
    forward(HERE, 1)
    forward(HERE, 2)
    quarter(HERE, 1, 0, 1, True)
    forward(HERE, 0)
    quarter(HERE, 1, 0, 0)
    from_partner(HERE, 1, 1)
    quarter(HERE, 1, 1, 1)
    from_partner(HERE, 1, 0)
    quarter(HERE, 1, 1, 0)
    terms(HERE, 1)
    last[24 + ga] = part[30]
    home(HERE, 1, last_ss.at[1], last_rs.at[1])
    arrived(res, res_rs)
    fin[ga] = jnp.sum(res[...], axis=0)
    for n, (gh, gc) in enumerate(((0, 1), (1, 0), (1, 1))):
        send(fin.at[ga], fin.at[ga], fin_ss.at[n], fin_rs, dev(0, 0, 0, gh, gc))
    arrived(fin.at[pl.ds(1, 3)], fin_rs)
    arrived(last.at[pl.ds(0, 24)], last_rs.at[0])
    arrived(last.at[pl.ds(25, 7)], last_rs.at[1])
    total = jnp.sum(fin[...], axis=0) + jnp.sum(last[...], axis=0)
    out_ref[...] = total[:, :16] / 64.0

    sent(d_send, con_ss.at[0])
    sent(s_send, con_ss.at[1])
    for n in range(3):
        sent(transit, relay_ss.at[n])
    for n in range(4):
        sent(transit, d2d_ss.at[n])
    sent(vs_send, val_ss.at[0])
    sent(vd_send, val_ss.at[1])
    sent(vs_send, val_ss.at[2])
    sent(qa_all.at[pl.ds(1, 31)], qa_ss)
    sent(res, res_ss)
    for n in range(3):
        sent(fin.at[0], fin_ss.at[n])
    sent(last.at[pl.ds(0, 24)], last_ss.at[0])
    sent(last.at[pl.ds(25, 7)], last_ss.at[1])


def body(pair_val, pair_con, screened, amplitude, qmap):
    bf16, f32, i32 = jnp.bfloat16, jnp.float32, jnp.int32
    block = (2, 2, 16, 512)
    dma = pltpu.SemaphoreType.DMA
    any_space = pl.BlockSpec(memory_space=pl.ANY)
    vmem = pl.BlockSpec(memory_space=pltpu.VMEM)
    return pl.pallas_call(
        kernel,
        out_shape=jax.ShapeDtypeStruct((2, 16), f32),
        in_specs=[any_space, any_space, any_space, vmem, vmem],
        out_specs=vmem,
        scratch_shapes=[
            pltpu.VMEM((2, 64, 16, 512), bf16),
            pltpu.VMEM((2, 64, 16, 512), bf16),
            pltpu.VMEM((2, 2048, 512), bf16),
            pltpu.VMEM((15, *block), bf16),
            pltpu.VMEM((15, *block), bf16),
            pltpu.VMEM((15, *block), bf16),
            pltpu.VMEM((16, *block), bf16),
            pltpu.VMEM((2, 2, 16, 2, *block), bf16),
            pltpu.VMEM((32, *block), bf16),
            pltpu.VMEM((16, *block), bf16),
            pltpu.VMEM((15, *block), bf16),
            pltpu.VMEM((2, 256, 512), f32),
            pltpu.VMEM((2, 1024, 256), bf16),
            pltpu.VMEM((2, 64), i32),
            pltpu.SMEM((2, 64), i32),
            pltpu.VMEM((32, 2, 128), f32),
            pltpu.VMEM((32, 2, 128), f32),
            pltpu.VMEM((24, 2, 128), f32),
            pltpu.VMEM((4, 2, 128), f32),
            pltpu.VMEM((32, 2, 128), f32),
            dma((4,)), dma((16,)), dma((16,)), dma((3, 16)), dma((4, 16)), dma((32,)), dma((16,)), dma, dma, dma, dma((2,)),
            dma((2,)), dma((3,)), dma((3,)), dma((4,)), dma, dma, dma((3,)), dma((2,)),
        ],
        compiler_params=pltpu.CompilerParams(collective_id=0, has_side_effects=True),
    )(pair_con, pair_val, screened, amplitude, qmap)


def solution(mesh):
    placed = (
        P("blk", None, None, "ga"),
        P("blk", None, None, "ga"),
        P("blk", None, "ga"),
        P("blk", None),
        P("blk", None),
    )
    return jax.shard_map(
        body, mesh=mesh, in_specs=placed, out_specs=P("blk", None), check_vma=False
    )
```

time: 110 us -> 90.9 us (0.83)
  Pallas kernels: 106 us -> 89.5 us
  other arithmetic: 3.34 us -> 0 us
    pallas_call x1, Pallas kernels: 106 us -> 89.5 us  [body(): pl.pallas_call(kernel, out_shape=jax.ShapeDtypeStruct((2, 16), f32), in_s...]
    reduce_sum x1 -> x0, other arithmetic: 1.34 us -> none  [inverse_rows(): return jnp.sum(hits * labels[None, :, None], axis=1)]
    convert_element_type x2 -> x0, other arithmetic: 1.34 us -> none  [the longest x1 0.68 us: body(): qmap.astype(jnp.float32)]
where the time goes in v2:
time: 90.9 us; the launch traced here: 90.8 us
  Pallas kernels  89.5 us (98%)
  local copies, waits for them, and re-layouts  1.24 us (1%)
    pallas_call x1, Pallas kernels, body(): pl.pallas_call(kernel, out_shape=jax.ShapeDtypeStruct((2, 16), f32), in_s...  89.5 us

profile of v2, /device:TPU:1, one launch (start us, length us, event | category | flops | bytes accessed | tf_op | source)
XLA Modules:
  0.0 90.8 jit_solution(8522390505826973137)
XLA Ops:
  0.0 89.5 %shard_map.55 = f32[2,16]{1,0:T(2,128)} custom-call(bf16[2,64,16,512]{3,2,1,0:T(8,128)(2,1)} %con_hbm.1, bf16[2,64,16,512]{3,2,1,0:T(8,128)(2,1)} %val_hbm.1, bf16[2,2048,512]{2,1,0:T(8,128)(2,1)} %w_hbm.1, bf16[2,16]{1,0:T(2,128)(2,1)} %amp_ref.1, s32[2,64]{1,0:T(2,128)} %qmap_ref.1), custom_call_target="tpu_custom_call" | custom-call | tf_op jit(solution)/shard_map/pallas_call | solution.py:294
  89.5 1.2 %copy.7 = f32[2,16]{1,0:T(2,128)} copy(f32[2,16]{1,0:T(2,128)} %shard_map.55) | data formatting | bytes 256

commit v3 on v2

--- a/solution.py
+++ b/solution.py
@@ -21,16 +21,11 @@
     return jnp.where(cond, 1.0, 0.0).astype(jnp.bfloat16)
 
 
-def hops(offset):
-    dx, dz, fl, gh, _ = offset
-    return min(dx, 4 - dx) + min(dz, 4 - dz) + (2 if gh and not fl else fl)
-
-
 def kernel(
     con_hbm, val_hbm, w_hbm, amp_ref, qmap_ref, out_ref,
     con_raw, val_raw, w, s_send, d_send, vs_send, vd_send, con_all, val_all, transit, val_transit,
     acc, weight, rows_ref, partner, qa_all, part, res, fin, last,
-    load_sem, s_rs, d_rs, y_rs, p_rs, val_rs, vt_rs, qa_rs, res_rs, fin_rs, last_rs,
+    ready, load_sem, s_rs, d_rs, y_rs, p_rs, val_rs, vt_rs, qa_rs, res_rs, fin_rs, last_rs,
     con_ss, val_ss, relay_ss, d2d_ss, qa_ss, res_ss, fin_ss, last_ss,
 ):
     blk, ga = lax.axis_index("blk"), lax.axis_index("ga")
@@ -48,16 +43,20 @@
         pltpu.make_async_copy(val_hbm, val_raw, load_sem.at[1]),
         pltpu.make_async_copy(w_hbm, w, load_sem.at[2]),
     ]
-    for load in loads:
-        load.start()
-
-    peers = {(dx, dz, fl, 0, 0) for dx, dz in ORDER for fl in (0, 1)}
-    peers |= {((4 - dx) % 4, (4 - dz) % 4, fl, gh, gc) for dx, dz in ORDER[12:] for fl in (0, 1) for gh in (0, 1) for gc in (0, 1)}
-    peers |= {(dx, dz, fl, gh, gc) for dx, dz in ORDER[12:] for fl in (0, 1) for gh in (0, 1) for gc in (0, 1)}
-    peers = sorted(peers - {(0, 0, 0, 0, 0)}, key=lambda p: (-hops(p), p))
+    along_x = [(d, 0, 0, 0, 0) for d in (2, 1, 3)]
+    along_z = [(0, d, 0, 0, 0) for d in (2, 1, 3)]
+    along_y = [(0, 0, 0, 1, 0), (0, 0, 1, 0, 0), (0, 0, 1, 1, 0)]
+    other_core = [(0, 0, 0, 0, 1)]
+    lines = along_x + along_z + along_y + other_core
     barrier = pltpu.get_barrier_semaphore()
-    for offset in peers:
+    for offset in lines:
         pl.semaphore_signal(barrier, inc=1, device_id=dev(*offset), device_id_type=MESH)
+    loads[1].start()
+    loads[0].start()
+
+    def tell(stage, group):
+        for offset in group:
+            pl.semaphore_signal(ready.at[stage], inc=1, device_id=dev(*offset), device_id_type=MESH)
 
     def send(src, dst, ss, rs, to):
         pltpu.make_async_remote_copy(src, dst, ss, rs, device_id=to, device_id_type=MESH).start()
@@ -80,61 +79,72 @@
     qa_all[blk] = moved + jnp.concatenate([qmap.astype(jnp.float32), jnp.zeros((2, 64), jnp.float32)], axis=1)
     to_smem.wait()
 
+    def ordered(raw, k, q, dx, dz, fl):
+        return raw[k, partner[k, dev(dx, dz, fl)[0] * 2 + q]]
+
+    loads[1].wait()
+    for fl, buffer in ((1, vd_send), (0, vs_send)):
+        for t, (dx, dz) in enumerate(ORDER):
+            for q in (0, 1):
+                for k in (0, 1):
+                    tile = ordered(val_raw, k, q, dx, dz, fl)
+                    if t == HERE and not fl:
+                        val_all[2 * HERE, q, k] = tile
+                    else:
+                        buffer[t, q, k] = tile
+    pl.semaphore_wait(barrier, len(lines))
+    tell(0, along_x)
+
+    def val_along_y(t):
+        if t == HERE:
+            send(vd_send.at[t], val_all.at[2 * t + 1], val_ss.at[1], val_rs.at[2 * t + 1], dev(0, 0, 1))
+        else:
+            send(vd_send.at[t], val_transit.at[t], val_ss.at[1], vt_rs.at[t], dev(0, 0, 1))
+
+    def val_onward(t):
+        arrived(val_transit.at[t], vt_rs.at[t])
+        send(val_transit.at[t], val_all.at[2 * t + 1], val_ss.at[2], val_rs.at[2 * t + 1], dev(*ORDER[t]))
+
+    for t in range(15):
+        val_along_y(t)
     loads[0].wait()
     for t, (dx, dz) in enumerate(ORDER):
         for fl, buffer in ((1, d_send), (0, s_send)):
-            first = dev(dx, dz, fl)[0] * 2
             for q in (0, 1):
                 for k in (0, 1):
-                    tile = con_raw[k, partner[k, first + q]]
+                    tile = ordered(con_raw, k, q, dx, dz, fl)
                     if t != HERE:
                         buffer[t, q, k] = tile
                     elif fl:
                         transit[HERE, q, k] = tile
                     else:
                         con_all[0, 0, HERE, 0, q, k] = tile
-    loads[1].wait()
-    for t, (dx, dz) in enumerate(ORDER):
-        for fl, buffer in ((1, vd_send), (0, vs_send)):
-            first = dev(dx, dz, fl)[0] * 2
-            for q in (0, 1):
-                for k in (0, 1):
-                    tile = val_raw[k, partner[k, first + q]]
-                    if t == HERE and not fl:
-                        val_all[2 * HERE, q, k] = tile
-                    else:
-                        buffer[t, q, k] = tile
-    pl.semaphore_wait(barrier, len(peers))
-
-    def val_along_y(t):
-        if t == HERE:
-            send(vd_send.at[t], val_all.at[2 * t + 1], val_ss.at[1], val_rs.at[2 * t + 1], dev(0, 0, 1))
-        else:
-            send(vd_send.at[t], val_transit.at[t], val_ss.at[1], vt_rs.at[t], dev(0, 0, 1))
-
-    def val_onward(t):
-        arrived(val_transit.at[t], vt_rs.at[t])
-        send(val_transit.at[t], val_all.at[2 * t + 1], val_ss.at[2], val_rs.at[2 * t + 1], dev(*ORDER[t]))
-
-    for t in range(16):
-        val_along_y(t)
+    loads[2].start()
+    pl.semaphore_wait(ready.at[0], 3)
+    tell(1, along_z)
     for block in range(0, 15, 4):
         for t in range(block, min(block + 4, 15)):
             send(d_send.at[t], transit.at[t], con_ss.at[0], d_rs.at[t], dev(*ORDER[t]))
         for t in range(block, min(block + 4, 15)):
             send(s_send.at[t], con_all.at[0, 0, t, 0], con_ss.at[1], s_rs.at[t], dev(*ORDER[t]))
+        if block == 4:
+            pl.semaphore_wait(ready.at[1], 3)
+            tell(2, other_core)
+            for t, (dx, dz) in enumerate(ORDER):
+                for fl in (0, 1):
+                    if t != HERE or fl:
+                        send(qa_all.at[blk], qa_all.at[blk], qa_ss, qa_rs, dev(dx, dz, fl))
     for t in range(15):
         send(vs_send.at[t], val_all.at[2 * t], val_ss.at[0], val_rs.at[2 * t], dev(*ORDER[t]))
-    for t, (dx, dz) in enumerate(ORDER):
-        for fl in (0, 1):
-            if t != HERE or fl:
-                send(qa_all.at[blk], qa_all.at[blk], qa_ss, qa_rs, dev(dx, dz, fl))
-
-    def relay(t):
+    pl.semaphore_wait(ready.at[2], 1)
+
+    def relay_d(t):
         if t != HERE:
             arrived(transit.at[t], d_rs.at[t])
         send(transit.at[t], con_all.at[0, 0, t, 1], relay_ss.at[0], y_rs.at[0, t], dev(0, 0, 1))
         send(transit.at[t], con_all.at[0, 1, t, 1], relay_ss.at[1], y_rs.at[1, t], dev(0, 0, 1, 1))
+
+    def relay_s(t):
         here = con_all.at[0, 0, t, 0]
         if t != HERE:
             arrived(here, s_rs.at[t])
@@ -227,41 +237,49 @@
                             slot = ((t - 12) * 2 + fl) * 4 + ga
                             send(part.at[t * 2 + fl], last.at[slot], ss, rs, dev(-dx, -dz, fl, gh, gc))
 
-    for t in range(16):
-        relay(t)
-        if t != HERE:
-            val_onward(t)
+    for t in range(15):
+        relay_d(t)
+        relay_s(t)
+        val_onward(t)
+    relay_s(HERE)
+    relay_d(HERE)
+    val_along_y(HERE)
     weights()
     loads[2].wait()
     for t in range(15):
         for n in range(3):
             forward(t, n)
-        if t in (5, 9, 13):
-            units(t - 5, 4)
-            terms(t - 5, 4)
-        if t == 13:
+        if t in (4, 8, 12):
+            units(t - 4, 4)
+            terms(t - 4, 4)
+        if t == 12:
             for u, (dx, dz) in enumerate(ORDER[:12]):
                 for fl in (0, 1):
                     send(part.at[u * 2 + fl], res.at[u * 2 + fl], res_ss, res_rs, dev(-dx, -dz, fl))
-    units(12, 3)
+    quarter(12, 3, 0, 0, True)
+    quarter(12, 3, 0, 1)
+    forward(HERE, 1)
+    forward(HERE, 2)
+    from_partner(12, 3, 0)
+    quarter(12, 3, 1, 0)
+    from_partner(12, 3, 1)
+    quarter(12, 3, 1, 1)
     terms(12, 3)
     home(12, 3, last_ss.at[0], last_rs.at[0])
-    forward(HERE, 1)
-    forward(HERE, 2)
+    forward(HERE, 0)
     quarter(HERE, 1, 0, 1, True)
-    forward(HERE, 0)
     quarter(HERE, 1, 0, 0)
     from_partner(HERE, 1, 1)
     quarter(HERE, 1, 1, 1)
+    arrived(res, res_rs)
+    fin[ga] = jnp.sum(res[...], axis=0)
+    for n, (gh, gc) in enumerate(((0, 1), (1, 0), (1, 1))):
+        send(fin.at[ga], fin.at[ga], fin_ss.at[n], fin_rs, dev(0, 0, 0, gh, gc))
     from_partner(HERE, 1, 0)
     quarter(HERE, 1, 1, 0)
     terms(HERE, 1)
     last[24 + ga] = part[30]
     home(HERE, 1, last_ss.at[1], last_rs.at[1])
-    arrived(res, res_rs)
-    fin[ga] = jnp.sum(res[...], axis=0)
-    for n, (gh, gc) in enumerate(((0, 1), (1, 0), (1, 1))):
-        send(fin.at[ga], fin.at[ga], fin_ss.at[n], fin_rs, dev(0, 0, 0, gh, gc))
     arrived(fin.at[pl.ds(1, 3)], fin_rs)
     arrived(last.at[pl.ds(0, 24)], last_rs.at[0])
     arrived(last.at[pl.ds(25, 7)], last_rs.at[1])
@@ -317,7 +335,7 @@
             pltpu.VMEM((24, 2, 128), f32),
             pltpu.VMEM((4, 2, 128), f32),
             pltpu.VMEM((32, 2, 128), f32),
-            dma((4,)), dma((16,)), dma((16,)), dma((3, 16)), dma((4, 16)), dma((32,)), dma((16,)), dma, dma, dma, dma((2,)),
+            pltpu.SemaphoreType.REGULAR((3,)), dma((4,)), dma((16,)), dma((16,)), dma((3, 16)), dma((4, 16)), dma((32,)), dma((16,)), dma, dma, dma, dma((2,)),
             dma((2,)), dma((3,)), dma((3,)), dma((4,)), dma, dma, dma((3,)), dma((2,)),
         ],
         compiler_params=pltpu.CompilerParams(collective_id=0, has_side_effects=True),

time: 90.9 us -> 87.6 us (0.964)
  Pallas kernels: 89.5 us -> 86.2 us
    pallas_call x1, Pallas kernels: 89.5 us -> 86.2 us  [body(): pl.pallas_call(kernel, out_shape=jax.ShapeDtypeStruct((2, 16), f32), in_s...]
where the time goes in v3:
time: 87.6 us; the launch traced here: 87.5 us
  Pallas kernels  86.2 us (98%)
  local copies, waits for them, and re-layouts  1.24 us (1%)
    pallas_call x1, Pallas kernels, body(): pl.pallas_call(kernel, out_shape=jax.ShapeDtypeStruct((2, 16), f32), in_s...  86.2 us

profile of v3, /device:TPU:1, one launch (start us, length us, event | category | flops | bytes accessed | tf_op | source)
XLA Modules:
  0.0 87.5 jit_solution(7956522762449022585)
XLA Ops:
  0.0 86.2 %shard_map.55 = f32[2,16]{1,0:T(2,128)} custom-call(bf16[2,64,16,512]{3,2,1,0:T(8,128)(2,1)} %con_hbm.1, bf16[2,64,16,512]{3,2,1,0:T(8,128)(2,1)} %val_hbm.1, bf16[2,2048,512]{2,1,0:T(8,128)(2,1)} %w_hbm.1, bf16[2,16]{1,0:T(2,128)(2,1)} %amp_ref.1, s32[2,64]{1,0:T(2,128)} %qmap_ref.1), custom_call_target="tpu_custom_call" | custom-call | tf_op jit(solution)/shard_map/pallas_call | solution.py:312
  86.2 1.2 %copy.7 = f32[2,16]{1,0:T(2,128)} copy(f32[2,16]{1,0:T(2,128)} %shard_map.55) | data formatting | bytes 256

commit v4 on v3

--- a/solution.py
+++ b/solution.py
@@ -8,8 +8,7 @@
 MESH = pl.DeviceIdType.MESH
 ORDER = ((2, 2), (1, 1), (3, 3), (1, 3), (3, 1), (2, 1), (1, 2), (2, 3), (3, 2), (2, 0), (0, 2), (0, 3), (1, 0), (3, 0), (0, 1), (0, 0))
 HERE = 15
-GROUPS = ((0, 4), (4, 4), (8, 4), (12, 3), (15, 1))
-QUARTERS = ((0, 0), (0, 1), (1, 0), (1, 1))
+GROUPS = ((0, 4), (4, 4), (8, 4), (12, 2), (14, 1), (15, 1))
 COLUMN = ((0, 1), (1, 1), (1, 0))
 
 
@@ -22,11 +21,11 @@
 
 
 def kernel(
-    con_hbm, val_hbm, w_hbm, amp_ref, qmap_ref, out_ref,
-    con_raw, val_raw, w, s_send, d_send, vs_send, vd_send, con_all, val_all, transit, val_transit,
-    acc, weight, rows_ref, partner, qa_all, part, res, fin, last,
-    ready, load_sem, s_rs, d_rs, y_rs, p_rs, val_rs, vt_rs, qa_rs, res_rs, fin_rs, last_rs,
-    con_ss, val_ss, relay_ss, d2d_ss, qa_ss, res_ss, fin_ss, last_ss,
+    con_hbm, val_hbm, w_hbm, amp_hbm, qmap_hbm, out_ref,
+    amp_ref, qmap_ref, con_raw, val_raw, w, s_send, d_send, vs_send, vd_send, con_all, val_all, transit, val_transit,
+    acc, weight, rows_ref, partner, qa_all, part, every,
+    ready, load_sem, s_rs, d_rs, y_rs, p_rs, val_rs, vt_rs, qa_rs, home_rs,
+    con_ss, val_ss, relay_ss, d2d_ss, qa_ss, home_ss,
 ):
     blk, ga = lax.axis_index("blk"), lax.axis_index("ga")
     lo, x, z = blk // 16, (blk // 4) % 4, blk % 4
@@ -42,17 +41,19 @@
         pltpu.make_async_copy(con_hbm, con_raw, load_sem.at[0]),
         pltpu.make_async_copy(val_hbm, val_raw, load_sem.at[1]),
         pltpu.make_async_copy(w_hbm, w, load_sem.at[2]),
+        pltpu.make_async_copy(qmap_hbm, qmap_ref, load_sem.at[3]),
+        pltpu.make_async_copy(amp_hbm, amp_ref, load_sem.at[4]),
     ]
     along_x = [(d, 0, 0, 0, 0) for d in (2, 1, 3)]
     along_z = [(0, d, 0, 0, 0) for d in (2, 1, 3)]
     along_y = [(0, 0, 0, 1, 0), (0, 0, 1, 0, 0), (0, 0, 1, 1, 0)]
     other_core = [(0, 0, 0, 0, 1)]
-    lines = along_x + along_z + along_y + other_core
+    lines = along_y + along_x + along_z + other_core
     barrier = pltpu.get_barrier_semaphore()
     for offset in lines:
         pl.semaphore_signal(barrier, inc=1, device_id=dev(*offset), device_id_type=MESH)
-    loads[1].start()
-    loads[0].start()
+    for n in (3, 4, 1, 0):
+        loads[n].start()
 
     def tell(stage, group):
         for offset in group:
@@ -66,14 +67,16 @@
 
     sent = arrived
 
+    loads[3].wait()
     qmap = qmap_ref[...]
     for k in (0, 1):
         hit = qmap[k : k + 1, :] == iota((64, 64), 0)
         column = jnp.max(jnp.where(hit, iota((64, 64), 1), 0), axis=1, keepdims=True)
         square = jnp.where(iota((64, 64), 0) == iota((64, 64), 1), column, 0)
         rows_ref[k : k + 1, :] = jnp.max(square, axis=0, keepdims=True)
-    to_smem = pltpu.make_async_copy(rows_ref, partner, load_sem.at[3])
+    to_smem = pltpu.make_async_copy(rows_ref, partner, load_sem.at[5])
     to_smem.start()
+    loads[4].wait()
     place = zero_one(iota((16, 128), 0) + 64 == iota((16, 128), 1))
     moved = jnp.dot(amp_ref[...], place, preferred_element_type=jnp.float32)
     qa_all[blk] = moved + jnp.concatenate([qmap.astype(jnp.float32), jnp.zeros((2, 64), jnp.float32)], axis=1)
@@ -158,8 +161,8 @@
 
     def weights():
         arrived(qa_all.at[pl.ds(1, 31)], qa_rs)
-        every = qa_all[...].reshape(64, 128)
-        amps = every.astype(jnp.bfloat16)
+        table = qa_all[...].reshape(64, 128)
+        amps = table.astype(jnp.bfloat16)
         pick = zero_one(iota((128, 128), 0) == iota((128, 128), 1) + 64)
         amps = jnp.dot(amps, pick, preferred_element_type=jnp.float32).astype(jnp.bfloat16)
         row = iota((64, 64), 0)
@@ -170,7 +173,7 @@
         perm = zero_one(source + row % 2 == iota((64, 64), 1))
         for q in (0, 1):
             mine = (blk * 2 + q).astype(jnp.float32)
-            hot = zero_one(every[:, :64] == mine)
+            hot = zero_one(table[:, :64] == mine)
             chosen = jnp.dot(hot, amps, preferred_element_type=jnp.float32).astype(jnp.bfloat16)
             chosen = jnp.dot(perm, chosen, preferred_element_type=jnp.float32).astype(jnp.bfloat16)
             spread = zero_one(iota((256, 16), 0) // 16 == iota((256, 16), 1))
@@ -203,11 +206,14 @@
 
         lax.fori_loop(0, 2, one, 0)
 
-    def units(t0, n):
-        for gc, gh in QUARTERS:
-            if gc:
-                from_partner(t0, n, gh)
-            quarter(t0, n, gc, gh, first=(gc, gh) == (0, 0))
+    def own(t0, n):
+        quarter(t0, n, 0, 0, True)
+        quarter(t0, n, 0, 1)
+
+    def others(t0, n):
+        for gh in (0, 1):
+            from_partner(t0, n, gh)
+            quarter(t0, n, 1, gh)
 
     def terms(t0, n):
         for t in range(t0, t0 + n):
@@ -222,20 +228,24 @@
             full = lax.dot_general(unit, vals, (((1,), (1,)), ((), ())), preferred_element_type=jnp.float32)
             total = total + full * weight[q, 64 * t0 : 64 * (t0 + n), :size].astype(jnp.float32)
         lanes = iota((size, 128), 1)
-        columns = jnp.where(((iota((size, 128), 0) // 4) % 4 == lanes // 4) & (lanes < 16), 1.0, 0.0)
-        summed = jnp.dot(total, columns, preferred_element_type=jnp.float32, precision=lax.Precision.HIGHEST)
+        columns = zero_one(((iota((size, 128), 0) // 4) % 4 == lanes // 4) & (lanes < 16))
+        high = total.astype(jnp.bfloat16)
+        low = (total - high.astype(jnp.float32)).astype(jnp.bfloat16)
+        summed = jnp.dot(high, columns, preferred_element_type=jnp.float32)
+        summed = summed + jnp.dot(low, columns, preferred_element_type=jnp.float32)
         summed = jnp.where((iota((size, 128), 0) // 4) % 4 == lanes % 4, summed, 0.0)
         part[2 * t0 : 2 * (t0 + n)] = jnp.sum(summed.reshape(4 * n, 16, 128), axis=1).reshape(2 * n, 2, 128)
 
-    def home(t0, n, ss, rs):
+    def home(t0, n):
+        batch = GROUPS.index((t0, n))
         for t in range(t0, t0 + n):
             dx, dz = ORDER[t]
             for fl in (0, 1):
                 for gh in (0, 1):
                     for gc in (0, 1):
                         if (dx, dz, fl, gh, gc) != (0, 0, 0, 0, 0):
-                            slot = ((t - 12) * 2 + fl) * 4 + ga
-                            send(part.at[t * 2 + fl], last.at[slot], ss, rs, dev(-dx, -dz, fl, gh, gc))
+                            slot = (t * 2 + fl) * 4 + ga
+                            send(part.at[t * 2 + fl], every.at[slot], home_ss.at[batch], home_rs.at[batch], dev(-dx, -dz, fl, gh, gc))
 
     for t in range(15):
         relay_d(t)
@@ -246,45 +256,41 @@
     val_along_y(HERE)
     weights()
     loads[2].wait()
-    for t in range(15):
+    for t in range(14):
         for n in range(3):
             forward(t, n)
+        if t in (3, 7, 11):
+            own(t - 3, 4)
         if t in (4, 8, 12):
-            units(t - 4, 4)
+            others(t - 4, 4)
             terms(t - 4, 4)
-        if t == 12:
-            for u, (dx, dz) in enumerate(ORDER[:12]):
-                for fl in (0, 1):
-                    send(part.at[u * 2 + fl], res.at[u * 2 + fl], res_ss, res_rs, dev(-dx, -dz, fl))
-    quarter(12, 3, 0, 0, True)
-    quarter(12, 3, 0, 1)
+            home(t - 4, 4)
+    own(12, 2)
+    others(12, 2)
+    terms(12, 2)
+    home(12, 2)
+    for n in range(3):
+        forward(14, n)
+    own(14, 1)
+    others(14, 1)
+    terms(14, 1)
+    home(14, 1)
     forward(HERE, 1)
     forward(HERE, 2)
-    from_partner(12, 3, 0)
-    quarter(12, 3, 1, 0)
-    from_partner(12, 3, 1)
-    quarter(12, 3, 1, 1)
-    terms(12, 3)
-    home(12, 3, last_ss.at[0], last_rs.at[0])
+    quarter(HERE, 1, 0, 1, True)
     forward(HERE, 0)
-    quarter(HERE, 1, 0, 1, True)
     quarter(HERE, 1, 0, 0)
     from_partner(HERE, 1, 1)
     quarter(HERE, 1, 1, 1)
-    arrived(res, res_rs)
-    fin[ga] = jnp.sum(res[...], axis=0)
-    for n, (gh, gc) in enumerate(((0, 1), (1, 0), (1, 1))):
-        send(fin.at[ga], fin.at[ga], fin_ss.at[n], fin_rs, dev(0, 0, 0, gh, gc))
     from_partner(HERE, 1, 0)
     quarter(HERE, 1, 1, 0)
     terms(HERE, 1)
-    last[24 + ga] = part[30]
-    home(HERE, 1, last_ss.at[1], last_rs.at[1])
-    arrived(fin.at[pl.ds(1, 3)], fin_rs)
-    arrived(last.at[pl.ds(0, 24)], last_rs.at[0])
-    arrived(last.at[pl.ds(25, 7)], last_rs.at[1])
-    total = jnp.sum(fin[...], axis=0) + jnp.sum(last[...], axis=0)
-    out_ref[...] = total[:, :16] / 64.0
+    every[120 + ga] = part[30]
+    home(HERE, 1)
+    for batch, (t0, n) in enumerate(GROUPS):
+        first = 8 * t0 + (t0 == HERE)
+        arrived(every.at[pl.ds(first, 8 * (t0 + n) - first)], home_rs.at[batch])
+    out_ref[...] = jnp.sum(every[...], axis=0)[:, :16] / 64.0
 
     sent(d_send, con_ss.at[0])
     sent(s_send, con_ss.at[1])
@@ -296,25 +302,25 @@
     sent(vd_send, val_ss.at[1])
     sent(vs_send, val_ss.at[2])
     sent(qa_all.at[pl.ds(1, 31)], qa_ss)
-    sent(res, res_ss)
-    for n in range(3):
-        sent(fin.at[0], fin_ss.at[n])
-    sent(last.at[pl.ds(0, 24)], last_ss.at[0])
-    sent(last.at[pl.ds(25, 7)], last_ss.at[1])
+    for batch, (t0, n) in enumerate(GROUPS):
+        first = 8 * t0 + (t0 == HERE)
+        sent(every.at[pl.ds(first, 8 * (t0 + n) - first)], home_ss.at[batch])
 
 
 def body(pair_val, pair_con, screened, amplitude, qmap):
     bf16, f32, i32 = jnp.bfloat16, jnp.float32, jnp.int32
     block = (2, 2, 16, 512)
     dma = pltpu.SemaphoreType.DMA
-    any_space = pl.BlockSpec(memory_space=pl.ANY)
+    hbm = pl.BlockSpec(memory_space=pl.ANY)
     vmem = pl.BlockSpec(memory_space=pltpu.VMEM)
     return pl.pallas_call(
         kernel,
         out_shape=jax.ShapeDtypeStruct((2, 16), f32),
-        in_specs=[any_space, any_space, any_space, vmem, vmem],
+        in_specs=[hbm] * 5,
         out_specs=vmem,
         scratch_shapes=[
+            pltpu.VMEM((2, 16), bf16),
+            pltpu.VMEM((2, 64), i32),
             pltpu.VMEM((2, 64, 16, 512), bf16),
             pltpu.VMEM((2, 64, 16, 512), bf16),
             pltpu.VMEM((2, 2048, 512), bf16),
@@ -332,11 +338,9 @@
             pltpu.SMEM((2, 64), i32),
             pltpu.VMEM((32, 2, 128), f32),
             pltpu.VMEM((32, 2, 128), f32),
-            pltpu.VMEM((24, 2, 128), f32),
-            pltpu.VMEM((4, 2, 128), f32),
-            pltpu.VMEM((32, 2, 128), f32),
-            pltpu.SemaphoreType.REGULAR((3,)), dma((4,)), dma((16,)), dma((16,)), dma((3, 16)), dma((4, 16)), dma((32,)), dma((16,)), dma, dma, dma, dma((2,)),
-            dma((2,)), dma((3,)), dma((3,)), dma((4,)), dma, dma, dma((3,)), dma((2,)),
+            pltpu.VMEM((128, 2, 128), f32),
+            pltpu.SemaphoreType.REGULAR((3,)), dma((6,)), dma((16,)), dma((16,)), dma((3, 16)), dma((4, 16)), dma((32,)), dma((16,)), dma, dma((6,)),
+            dma((2,)), dma((3,)), dma((3,)), dma((4,)), dma, dma((6,)),
         ],
         compiler_params=pltpu.CompilerParams(collective_id=0, has_side_effects=True),
     )(pair_con, pair_val, screened, amplitude, qmap)

time: 87.6 us -> 85.4 us (0.975)
  Pallas kernels: 86.2 us -> 84 us
    pallas_call x1, Pallas kernels: 86.2 us -> 84 us  [body(): pl.pallas_call(kernel, out_shape=jax.ShapeDtypeStruct((2, 16), f32), in_s...]
where the time goes in v4:
time: 85.4 us; the launch traced here: 85.2 us
  Pallas kernels  84 us (98%)
  local copies, waits for them, and re-layouts  1.24 us (1%)
    pallas_call x1, Pallas kernels, body(): pl.pallas_call(kernel, out_shape=jax.ShapeDtypeStruct((2, 16), f32), in_s...  84 us

profile of v4, /device:TPU:1, one launch (start us, length us, event | category | flops | bytes accessed | tf_op | source)
XLA Modules:
  0.0 85.2 jit_solution(6536882109189015476)
XLA Ops:
  0.0 84.0 %shard_map.55 = f32[2,16]{1,0:T(2,128)} custom-call(bf16[2,64,16,512]{3,2,1,0:T(8,128)(2,1)} %con_hbm.1, bf16[2,64,16,512]{3,2,1,0:T(8,128)(2,1)} %val_hbm.1, bf16[2,2048,512]{2,1,0:T(8,128)(2,1)} %w_hbm.1, bf16[2,16]{1,0:T(2,128)(2,1)} %amp_hbm.1, s32[2,64]{1,0:T(2,128)} %qmap_hbm.1), custom_call_target="tpu_custom_call" | custom-call | tf_op jit(solution)/shard_map/pallas_call | solution.py:316
  84.0 1.2 %copy.7 = f32[2,16]{1,0:T(2,128)} copy(f32[2,16]{1,0:T(2,128)} %shard_map.55) | data formatting | bytes 256

commit v5 on v4

--- a/solution.py
+++ b/solution.py
@@ -21,11 +21,11 @@
 
 
 def kernel(
-    con_hbm, val_hbm, w_hbm, amp_hbm, qmap_hbm, out_ref,
-    amp_ref, qmap_ref, con_raw, val_raw, w, s_send, d_send, vs_send, vd_send, con_all, val_all, transit, val_transit,
-    acc, weight, rows_ref, partner, qa_all, part, every,
-    ready, load_sem, s_rs, d_rs, y_rs, p_rs, val_rs, vt_rs, qa_rs, home_rs,
-    con_ss, val_ss, relay_ss, d2d_ss, qa_ss, home_ss,
+    con_hbm, val_hbm, w_hbm, amp_ref, qmap_hbm, out_ref,
+    qmap_ref, con_raw, val_raw, w, s_send, d_send, vs_send, vd_send, con_all, val_all, transit, val_transit,
+    acc, weight, rows_ref, partner, qa_all, part, gathered, fin, crossing,
+    ready, load_sem, s_rs, d_rs, y_rs, p_rs, val_rs, vt_rs, qa_rs, home_rs, fin_rs,
+    con_ss, val_ss, relay_ss, d2d_ss, qa_ss, home_ss, fin_ss,
 ):
     blk, ga = lax.axis_index("blk"), lax.axis_index("ga")
     lo, x, z = blk // 16, (blk // 4) % 4, blk % 4
@@ -42,7 +42,6 @@
         pltpu.make_async_copy(val_hbm, val_raw, load_sem.at[1]),
         pltpu.make_async_copy(w_hbm, w, load_sem.at[2]),
         pltpu.make_async_copy(qmap_hbm, qmap_ref, load_sem.at[3]),
-        pltpu.make_async_copy(amp_hbm, amp_ref, load_sem.at[4]),
     ]
     along_x = [(d, 0, 0, 0, 0) for d in (2, 1, 3)]
     along_z = [(0, d, 0, 0, 0) for d in (2, 1, 3)]
@@ -52,12 +51,12 @@
     barrier = pltpu.get_barrier_semaphore()
     for offset in lines:
         pl.semaphore_signal(barrier, inc=1, device_id=dev(*offset), device_id_type=MESH)
-    for n in (3, 4, 1, 0):
+    for n in (3, 1, 0):
         loads[n].start()
 
-    def tell(stage, group):
+    def tell(group):
         for offset in group:
-            pl.semaphore_signal(ready.at[stage], inc=1, device_id=dev(*offset), device_id_type=MESH)
+            pl.semaphore_signal(ready, inc=1, device_id=dev(*offset), device_id_type=MESH)
 
     def send(src, dst, ss, rs, to):
         pltpu.make_async_remote_copy(src, dst, ss, rs, device_id=to, device_id_type=MESH).start()
@@ -76,7 +75,6 @@
         rows_ref[k : k + 1, :] = jnp.max(square, axis=0, keepdims=True)
     to_smem = pltpu.make_async_copy(rows_ref, partner, load_sem.at[5])
     to_smem.start()
-    loads[4].wait()
     place = zero_one(iota((16, 128), 0) + 64 == iota((16, 128), 1))
     moved = jnp.dot(amp_ref[...], place, preferred_element_type=jnp.float32)
     qa_all[blk] = moved + jnp.concatenate([qmap.astype(jnp.float32), jnp.zeros((2, 64), jnp.float32)], axis=1)
@@ -96,7 +94,7 @@
                     else:
                         buffer[t, q, k] = tile
     pl.semaphore_wait(barrier, len(lines))
-    tell(0, along_x)
+    tell(along_x + other_core)
 
     def val_along_y(t):
         if t == HERE:
@@ -123,24 +121,17 @@
                     else:
                         con_all[0, 0, HERE, 0, q, k] = tile
     loads[2].start()
-    pl.semaphore_wait(ready.at[0], 3)
-    tell(1, along_z)
+    pl.semaphore_wait(ready, 4)
     for block in range(0, 15, 4):
         for t in range(block, min(block + 4, 15)):
             send(d_send.at[t], transit.at[t], con_ss.at[0], d_rs.at[t], dev(*ORDER[t]))
         for t in range(block, min(block + 4, 15)):
             send(s_send.at[t], con_all.at[0, 0, t, 0], con_ss.at[1], s_rs.at[t], dev(*ORDER[t]))
         if block == 4:
-            pl.semaphore_wait(ready.at[1], 3)
-            tell(2, other_core)
-            for t, (dx, dz) in enumerate(ORDER):
-                for fl in (0, 1):
-                    if t != HERE or fl:
-                        send(qa_all.at[blk], qa_all.at[blk], qa_ss, qa_rs, dev(dx, dz, fl))
+            for t in range(15):
+                send(qa_all.at[blk], qa_all.at[blk], qa_ss.at[0], qa_rs.at[0], dev(*ORDER[t]))
     for t in range(15):
         send(vs_send.at[t], val_all.at[2 * t], val_ss.at[0], val_rs.at[2 * t], dev(*ORDER[t]))
-    pl.semaphore_wait(ready.at[2], 1)
-
     def relay_d(t):
         if t != HERE:
             arrived(transit.at[t], d_rs.at[t])
@@ -160,7 +151,7 @@
         send(con_all.at[0, gh, t, fl], con_all.at[1, gh, t, fl], d2d_ss.at[n], p_rs.at[n, t], dev(0, 0, 0, 0, 1))
 
     def weights():
-        arrived(qa_all.at[pl.ds(1, 31)], qa_rs)
+        arrived(qa_all.at[pl.ds(0, 16)], qa_rs.at[1])
         table = qa_all[...].reshape(64, 128)
         amps = table.astype(jnp.bfloat16)
         pick = zero_one(iota((128, 128), 0) == iota((128, 128), 1) + 64)
@@ -234,23 +225,21 @@
         summed = jnp.dot(high, columns, preferred_element_type=jnp.float32)
         summed = summed + jnp.dot(low, columns, preferred_element_type=jnp.float32)
         summed = jnp.where((iota((size, 128), 0) // 4) % 4 == lanes % 4, summed, 0.0)
-        part[2 * t0 : 2 * (t0 + n)] = jnp.sum(summed.reshape(4 * n, 16, 128), axis=1).reshape(2 * n, 2, 128)
+        part[t0 : t0 + n] = jnp.sum(summed.reshape(4 * n, 16, 128), axis=1).reshape(n, 2, 2, 128)
 
     def home(t0, n):
-        batch = GROUPS.index((t0, n))
         for t in range(t0, t0 + n):
             dx, dz = ORDER[t]
-            for fl in (0, 1):
-                for gh in (0, 1):
-                    for gc in (0, 1):
-                        if (dx, dz, fl, gh, gc) != (0, 0, 0, 0, 0):
-                            slot = (t * 2 + fl) * 4 + ga
-                            send(part.at[t * 2 + fl], every.at[slot], home_ss.at[batch], home_rs.at[batch], dev(-dx, -dz, fl, gh, gc))
+            send(part.at[t], gathered.at[t], home_ss, home_rs, dev(-dx, -dz))
 
     for t in range(15):
         relay_d(t)
         relay_s(t)
         val_onward(t)
+        if t == 2:
+            arrived(qa_all.at[pl.ds(0, 15)], qa_rs.at[0])
+            plane = qa_all.at[pl.ds(lo * 16, 16)]
+            send(plane, plane, qa_ss.at[1], qa_rs.at[1], dev(0, 0, 1))
     relay_s(HERE)
     relay_d(HERE)
     val_along_y(HERE)
@@ -285,12 +274,17 @@
     from_partner(HERE, 1, 0)
     quarter(HERE, 1, 1, 0)
     terms(HERE, 1)
-    every[120 + ga] = part[30]
-    home(HERE, 1)
-    for batch, (t0, n) in enumerate(GROUPS):
-        first = 8 * t0 + (t0 == HERE)
-        arrived(every.at[pl.ds(first, 8 * (t0 + n) - first)], home_rs.at[batch])
-    out_ref[...] = jnp.sum(every[...], axis=0)[:, :16] / 64.0
+    arrived(gathered, home_rs)
+    column = part[HERE] + jnp.sum(gathered[...], axis=0)
+    fin[ga] = column[0]
+    crossing[...] = column[1]
+    for gh in (0, 1):
+        for gc in (0, 1):
+            send(crossing, fin.at[4 + ga], fin_ss, fin_rs, dev(0, 0, 1, gh, gc))
+            if (gh, gc) != (0, 0):
+                send(fin.at[ga], fin.at[ga], fin_ss, fin_rs, dev(0, 0, 0, gh, gc))
+    arrived(fin.at[pl.ds(1, 7)], fin_rs)
+    out_ref[...] = jnp.sum(fin[...], axis=0)[:, :16] / 64.0
 
     sent(d_send, con_ss.at[0])
     sent(s_send, con_ss.at[1])
@@ -301,10 +295,10 @@
     sent(vs_send, val_ss.at[0])
     sent(vd_send, val_ss.at[1])
     sent(vs_send, val_ss.at[2])
-    sent(qa_all.at[pl.ds(1, 31)], qa_ss)
-    for batch, (t0, n) in enumerate(GROUPS):
-        first = 8 * t0 + (t0 == HERE)
-        sent(every.at[pl.ds(first, 8 * (t0 + n) - first)], home_ss.at[batch])
+    sent(qa_all.at[pl.ds(0, 15)], qa_ss.at[0])
+    sent(qa_all.at[pl.ds(0, 16)], qa_ss.at[1])
+    sent(gathered, home_ss)
+    sent(fin.at[pl.ds(1, 7)], fin_ss)
 
 
 def body(pair_val, pair_con, screened, amplitude, qmap):
@@ -316,10 +310,9 @@
     return pl.pallas_call(
         kernel,
         out_shape=jax.ShapeDtypeStruct((2, 16), f32),
-        in_specs=[hbm] * 5,
+        in_specs=[hbm, hbm, hbm, vmem, hbm],
         out_specs=vmem,
         scratch_shapes=[
-            pltpu.VMEM((2, 16), bf16),
             pltpu.VMEM((2, 64), i32),
             pltpu.VMEM((2, 64, 16, 512), bf16),
             pltpu.VMEM((2, 64, 16, 512), bf16),
@@ -337,12 +330,14 @@
             pltpu.VMEM((2, 64), i32),
             pltpu.SMEM((2, 64), i32),
             pltpu.VMEM((32, 2, 128), f32),
-            pltpu.VMEM((32, 2, 128), f32),
-            pltpu.VMEM((128, 2, 128), f32),
-            pltpu.SemaphoreType.REGULAR((3,)), dma((6,)), dma((16,)), dma((16,)), dma((3, 16)), dma((4, 16)), dma((32,)), dma((16,)), dma, dma((6,)),
-            dma((2,)), dma((3,)), dma((3,)), dma((4,)), dma, dma((6,)),
+            pltpu.VMEM((16, 2, 2, 128), f32),
+            pltpu.VMEM((15, 2, 2, 128), f32),
+            pltpu.VMEM((8, 2, 128), f32),
+            pltpu.VMEM((2, 128), f32),
+            pltpu.SemaphoreType.REGULAR, dma((6,)), dma((16,)), dma((16,)), dma((3, 16)), dma((4, 16)), dma((32,)), dma((16,)), dma((2,)), dma, dma,
+            dma((2,)), dma((3,)), dma((3,)), dma((4,)), dma((2,)), dma, dma,
         ],
-        compiler_params=pltpu.CompilerParams(collective_id=0, has_side_effects=True),
+        compiler_params=pltpu.CompilerParams(collective_id=0, has_side_effects=True, vmem_limit_bytes=55224 * 1024),
     )(pair_con, pair_val, screened, amplitude, qmap)
 
 

time: 85.4 us -> 83.8 us (0.981)
  Pallas kernels: 84 us -> 82.5 us
    pallas_call x1, Pallas kernels: 84 us -> 82.5 us  [body(): pl.pallas_call(kernel, out_shape=jax.ShapeDtypeStruct((2, 16), f32), in_s...]
where the time goes in v5:
time: 83.8 us; the launch traced here: 83.7 us
  Pallas kernels  82.5 us (98%)
  local copies, waits for them, and re-layouts  1.22 us (1%)
    pallas_call x1, Pallas kernels, body(): pl.pallas_call(kernel, out_shape=jax.ShapeDtypeStruct((2, 16), f32), in_s...  82.5 us

profile of v5, /device:TPU:1, one launch (start us, length us, event | category | flops | bytes accessed | tf_op | source)
XLA Modules:
  0.0 83.7 jit_solution(6461323584909736015)
XLA Ops:
  0.0 0.0 copy-start
  0.0 0.7 copy-done
  0.7 82.5 %shard_map.55 = f32[2,16]{1,0:T(2,128)S(1)} custom-call(bf16[2,64,16,512]{3,2,1,0:T(8,128)(2,1)} %con_hbm.1, bf16[2,64,16,512]{3,2,1,0:T(8,128)(2,1)} %val_hbm.1, bf16[2,2048,512]{2,1,0:T(8,128)(2,1)} %w_hbm.1, bf16[2,16]{1,0:T(2,128)(2,1)S(1)} %copy-done, s32[2,64]{1,0:T(2,128)} %qmap_hbm.1), custom_call_target="tpu_custom_call" | custom-call | tf_op jit(solution)/shard_map/pallas_call | solution.py:310
  83.2 0.6 copy.7
Async XLA Ops:
  0.0 0.7 copy-start

commit v6 on v5

--- a/solution.py
+++ b/solution.py
@@ -9,7 +9,13 @@
 ORDER = ((2, 2), (1, 1), (3, 3), (1, 3), (3, 1), (2, 1), (1, 2), (2, 3), (3, 2), (2, 0), (0, 2), (0, 3), (1, 0), (3, 0), (0, 1), (0, 0))
 HERE = 15
 GROUPS = ((0, 4), (4, 4), (8, 4), (12, 2), (14, 1), (15, 1))
-COLUMN = ((0, 1), (1, 1), (1, 0))
+Y_OF = (0, 0, 1, 1, 2, 2, 3, 3, 4, 4, 5, 5, 6, 7, 8, 9)
+LO_OF = Y_OF[:15] + (10,)
+PARTNER_OF = ((0, 0),) * 4 + ((1, 1),) * 4 + ((2, 2),) * 4 + ((3, 3),) * 2 + ((4, 4),) + ((5, 6),)
+
+
+def group_of(t):
+    return [t0 <= t < t0 + n for t0, n in GROUPS].index(True)
 
 
 def iota(shape, dim):
@@ -24,8 +30,8 @@
     con_hbm, val_hbm, w_hbm, amp_ref, qmap_hbm, out_ref,
     qmap_ref, con_raw, val_raw, w, s_send, d_send, vs_send, vd_send, con_all, val_all, transit, val_transit,
     acc, weight, rows_ref, partner, qa_all, part, gathered, fin, crossing,
-    ready, load_sem, s_rs, d_rs, y_rs, p_rs, val_rs, vt_rs, qa_rs, home_rs, fin_rs,
-    con_ss, val_ss, relay_ss, d2d_ss, qa_ss, home_ss, fin_ss,
+    ready, load_sem, con_rs, y_rs, p_rs, val_rs, vt_rs, qa_rs, home_rs, fin_rs,
+    con_ss, vd_ss, val_ss, relay_ss, d2d_ss, qa_ss, home_ss, fin_ss,
 ):
     blk, ga = lax.axis_index("blk"), lax.axis_index("ga")
     lo, x, z = blk // 16, (blk // 4) % 4, blk % 4
@@ -40,8 +46,8 @@
     loads = [
         pltpu.make_async_copy(con_hbm, con_raw, load_sem.at[0]),
         pltpu.make_async_copy(val_hbm, val_raw, load_sem.at[1]),
-        pltpu.make_async_copy(w_hbm, w, load_sem.at[2]),
-        pltpu.make_async_copy(qmap_hbm, qmap_ref, load_sem.at[3]),
+        pltpu.make_async_copy(w_hbm, w, load_sem.at[1]),
+        pltpu.make_async_copy(qmap_hbm, qmap_ref, load_sem.at[2]),
     ]
     along_x = [(d, 0, 0, 0, 0) for d in (2, 1, 3)]
     along_z = [(0, d, 0, 0, 0) for d in (2, 1, 3)]
@@ -73,7 +79,7 @@
         column = jnp.max(jnp.where(hit, iota((64, 64), 1), 0), axis=1, keepdims=True)
         square = jnp.where(iota((64, 64), 0) == iota((64, 64), 1), column, 0)
         rows_ref[k : k + 1, :] = jnp.max(square, axis=0, keepdims=True)
-    to_smem = pltpu.make_async_copy(rows_ref, partner, load_sem.at[5])
+    to_smem = pltpu.make_async_copy(rows_ref, partner, load_sem.at[2])
     to_smem.start()
     place = zero_one(iota((16, 128), 0) + 64 == iota((16, 128), 1))
     moved = jnp.dot(amp_ref[...], place, preferred_element_type=jnp.float32)
@@ -97,16 +103,16 @@
     tell(along_x + other_core)
 
     def val_along_y(t):
-        if t == HERE:
-            send(vd_send.at[t], val_all.at[2 * t + 1], val_ss.at[1], val_rs.at[2 * t + 1], dev(0, 0, 1))
-        else:
-            send(vd_send.at[t], val_transit.at[t], val_ss.at[1], vt_rs.at[t], dev(0, 0, 1))
+        some = pl.ds(t, 3)
+        send(vd_send.at[some], val_transit.at[some], vd_ss, vt_rs.at[t // 3], dev(0, 0, 1))
 
     def val_onward(t):
-        arrived(val_transit.at[t], vt_rs.at[t])
-        send(val_transit.at[t], val_all.at[2 * t + 1], val_ss.at[2], val_rs.at[2 * t + 1], dev(*ORDER[t]))
-
-    for t in range(15):
+        some = pl.ds(t, 3)
+        arrived(val_transit.at[some], vt_rs.at[t // 3])
+        for u in range(t, t + 3):
+            send(val_transit.at[u], val_all.at[2 * u + 1], val_ss, val_rs.at[group_of(u)], dev(*ORDER[u]))
+
+    for t in range(0, 15, 3):
         val_along_y(t)
     loads[0].wait()
     for t, (dx, dz) in enumerate(ORDER):
@@ -122,33 +128,29 @@
                         con_all[0, 0, HERE, 0, q, k] = tile
     loads[2].start()
     pl.semaphore_wait(ready, 4)
+    for t in range(15):
+        send(qa_all.at[blk], qa_all.at[blk], qa_ss, qa_rs.at[0], dev(*ORDER[t]))
     for block in range(0, 15, 4):
         for t in range(block, min(block + 4, 15)):
-            send(d_send.at[t], transit.at[t], con_ss.at[0], d_rs.at[t], dev(*ORDER[t]))
+            send(d_send.at[t], transit.at[t], con_ss, con_rs.at[t // 2], dev(*ORDER[t]))
         for t in range(block, min(block + 4, 15)):
-            send(s_send.at[t], con_all.at[0, 0, t, 0], con_ss.at[1], s_rs.at[t], dev(*ORDER[t]))
-        if block == 4:
-            for t in range(15):
-                send(qa_all.at[blk], qa_all.at[blk], qa_ss.at[0], qa_rs.at[0], dev(*ORDER[t]))
+            send(s_send.at[t], con_all.at[0, 0, t, 0], con_ss, con_rs.at[t // 2], dev(*ORDER[t]))
     for t in range(15):
-        send(vs_send.at[t], val_all.at[2 * t], val_ss.at[0], val_rs.at[2 * t], dev(*ORDER[t]))
-    def relay_d(t):
-        if t != HERE:
-            arrived(transit.at[t], d_rs.at[t])
-        send(transit.at[t], con_all.at[0, 0, t, 1], relay_ss.at[0], y_rs.at[0, t], dev(0, 0, 1))
-        send(transit.at[t], con_all.at[0, 1, t, 1], relay_ss.at[1], y_rs.at[1, t], dev(0, 0, 1, 1))
-
-    def relay_s(t):
-        here = con_all.at[0, 0, t, 0]
-        if t != HERE:
-            arrived(here, s_rs.at[t])
-        send(here, con_all.at[0, 1, t, 0], relay_ss.at[2], y_rs.at[2, t], dev(0, 0, 0, 1))
-        send(here, con_all.at[1, 0, t, 0], d2d_ss.at[3], p_rs.at[3, t], dev(0, 0, 0, 0, 1))
-
-    def forward(t, n):
-        gh, fl = COLUMN[n]
-        arrived(con_all.at[0, gh, t, fl], y_rs.at[n, t])
-        send(con_all.at[0, gh, t, fl], con_all.at[1, gh, t, fl], d2d_ss.at[n], p_rs.at[n, t], dev(0, 0, 0, 0, 1))
+        send(vs_send.at[t], val_all.at[2 * t], val_ss, val_rs.at[group_of(t)], dev(*ORDER[t]))
+
+    def relay(t):
+        send(transit.at[t], con_all.at[0, 0, t, 1], relay_ss, y_rs.at[LO_OF[t]], dev(0, 0, 1))
+        send(transit.at[t], con_all.at[0, 1, t, 1], relay_ss, y_rs.at[Y_OF[t]], dev(0, 0, 1, 1))
+        send(con_all.at[0, 0, t, 0], con_all.at[0, 1, t, 0], relay_ss, y_rs.at[Y_OF[t]], dev(0, 0, 0, 1))
+
+    def forward(t, n, gh):
+        some = con_all.at[0, gh, pl.ds(t, n)]
+        send(some, con_all.at[1, gh, pl.ds(t, n)], d2d_ss, p_rs.at[PARTNER_OF[t][gh]], dev(0, 0, 0, 0, 1))
+
+    def come(t, n):
+        arrived(val_all.at[pl.ds(0, 3 * n)], y_rs.at[Y_OF[t]])
+        for gh in (0, 1):
+            forward(t, n, gh)
 
     def weights():
         arrived(qa_all.at[pl.ds(0, 16)], qa_rs.at[1])
@@ -176,12 +178,6 @@
                 same = iota((64 * n, 256), 0) // 16 == iota((64 * n, 256), 1) // 16
                 weight[q, 64 * t0 : 64 * (t0 + n)] = jnp.where(same, full, 0.0).astype(jnp.bfloat16)
 
-    def from_partner(t0, n, gh):
-        for t in range(t0, t0 + n):
-            for m, (of_h, fl) in enumerate(COLUMN + ((0, 0),)):
-                if of_h == gh:
-                    arrived(con_all.at[1, gh, t, fl], p_rs.at[m, t])
-
     def quarter(t0, n, gc, gh, first=False):
         g = ((h + gh) % 2) * 2 + (c + gc) % 2
 
@@ -202,15 +198,14 @@
         quarter(t0, n, 0, 1)
 
     def others(t0, n):
-        for gh in (0, 1):
-            from_partner(t0, n, gh)
-            quarter(t0, n, 1, gh)
+        arrived(con_all.at[1, :, pl.ds(t0, n)], p_rs.at[PARTNER_OF[t0][0]])
+        quarter(t0, n, 1, 0)
+        quarter(t0, n, 1, 1)
 
     def terms(t0, n):
-        for t in range(t0, t0 + n):
-            for fl in (0, 1):
-                if t != HERE or fl:
-                    arrived(val_all.at[t * 2 + fl], val_rs.at[t * 2 + fl])
+        first = 2 * t0 + (t0 == HERE)
+        some = pl.ds(first, 2 * (t0 + n) - first)
+        arrived(val_all.at[some], val_rs.at[group_of(t0)])
         size = 64 * n
         total = jnp.zeros((size, size), jnp.float32)
         for q in (0, 1):
@@ -233,45 +228,50 @@
             send(part.at[t], gathered.at[t], home_ss, home_rs, dev(-dx, -dz))
 
     for t in range(15):
-        relay_d(t)
-        relay_s(t)
-        val_onward(t)
-        if t == 2:
+        if t % 2 == 0:
+            n = min(2, 15 - t)
+            arrived(con_all.at[0, 0, pl.ds(t, n)], con_rs.at[t // 2])
+        relay(t)
+        if t == 3:
             arrived(qa_all.at[pl.ds(0, 15)], qa_rs.at[0])
             plane = qa_all.at[pl.ds(lo * 16, 16)]
-            send(plane, plane, qa_ss.at[1], qa_rs.at[1], dev(0, 0, 1))
-    relay_s(HERE)
-    relay_d(HERE)
-    val_along_y(HERE)
+            send(plane, plane, qa_ss, qa_rs.at[1], dev(0, 0, 1))
+        if t % 3 == 2:
+            val_onward(t - 2)
     weights()
     loads[2].wait()
-    for t in range(14):
-        for n in range(3):
-            forward(t, n)
-        if t in (3, 7, 11):
-            own(t - 3, 4)
+    for t in range(0, 14, 2):
+        if t < 12:
+            come(t, 2)
+        else:
+            come(12, 1)
         if t in (4, 8, 12):
             others(t - 4, 4)
             terms(t - 4, 4)
             home(t - 4, 4)
+        if t in (2, 6, 10):
+            own(t - 2, 4)
+    come(13, 1)
+    relay(HERE)
+    send(vd_send.at[HERE], val_all.at[2 * HERE + 1], vd_ss, val_rs.at[group_of(HERE)], dev(0, 0, 1))
     own(12, 2)
     others(12, 2)
     terms(12, 2)
     home(12, 2)
-    for n in range(3):
-        forward(14, n)
+    come(14, 1)
     own(14, 1)
     others(14, 1)
     terms(14, 1)
     home(14, 1)
-    forward(HERE, 1)
-    forward(HERE, 2)
+    arrived(con_all.at[0, 1, HERE], y_rs.at[Y_OF[HERE]])
+    forward(HERE, 1, 1)
     quarter(HERE, 1, 0, 1, True)
-    forward(HERE, 0)
+    arrived(con_all.at[0, 0, HERE, 1], y_rs.at[LO_OF[HERE]])
+    forward(HERE, 1, 0)
     quarter(HERE, 1, 0, 0)
-    from_partner(HERE, 1, 1)
+    arrived(con_all.at[1, 1, HERE], p_rs.at[PARTNER_OF[HERE][1]])
     quarter(HERE, 1, 1, 1)
-    from_partner(HERE, 1, 0)
+    arrived(con_all.at[1, 0, HERE], p_rs.at[PARTNER_OF[HERE][0]])
     quarter(HERE, 1, 1, 0)
     terms(HERE, 1)
     arrived(gathered, home_rs)
@@ -286,17 +286,12 @@
     arrived(fin.at[pl.ds(1, 7)], fin_rs)
     out_ref[...] = jnp.sum(fin[...], axis=0)[:, :16] / 64.0
 
-    sent(d_send, con_ss.at[0])
-    sent(s_send, con_ss.at[1])
-    for n in range(3):
-        sent(transit, relay_ss.at[n])
-    for n in range(4):
-        sent(transit, d2d_ss.at[n])
-    sent(vs_send, val_ss.at[0])
-    sent(vd_send, val_ss.at[1])
-    sent(vs_send, val_ss.at[2])
-    sent(qa_all.at[pl.ds(0, 15)], qa_ss.at[0])
-    sent(qa_all.at[pl.ds(0, 16)], qa_ss.at[1])
+    sent(val_all.at[pl.ds(0, 30)], con_ss)
+    sent(con_all.at[0, :, pl.ds(0, 12)], relay_ss)
+    sent(con_all.at[0], d2d_ss)
+    sent(vd_send, vd_ss)
+    sent(val_all.at[pl.ds(0, 30)], val_ss)
+    sent(qa_all.at[pl.ds(0, 31)], qa_ss)
     sent(gathered, home_ss)
     sent(fin.at[pl.ds(1, 7)], fin_ss)
 
@@ -334,8 +329,8 @@
             pltpu.VMEM((15, 2, 2, 128), f32),
             pltpu.VMEM((8, 2, 128), f32),
             pltpu.VMEM((2, 128), f32),
-            pltpu.SemaphoreType.REGULAR, dma((6,)), dma((16,)), dma((16,)), dma((3, 16)), dma((4, 16)), dma((32,)), dma((16,)), dma((2,)), dma, dma,
-            dma((2,)), dma((3,)), dma((3,)), dma((4,)), dma((2,)), dma, dma,
+            pltpu.SemaphoreType.REGULAR, dma((3,)), dma((8,)), dma((11,)), dma((7,)), dma((6,)), dma((5,)), dma((2,)), dma, dma,
+            dma, dma, dma, dma, dma, dma, dma, dma,
         ],
         compiler_params=pltpu.CompilerParams(collective_id=0, has_side_effects=True, vmem_limit_bytes=55224 * 1024),
     )(pair_con, pair_val, screened, amplitude, qmap)

time: 83.8 us -> 82.6 us (0.986)
  Pallas kernels: 82.5 us -> 81.2 us
    pallas_call x1, Pallas kernels: 82.5 us -> 81.2 us  [body(): pl.pallas_call(kernel, out_shape=jax.ShapeDtypeStruct((2, 16), f32), in_s...]
where the time goes in v6:
time: 82.6 us; the launch traced here: 82.5 us
  Pallas kernels  81.2 us (98%)
  local copies, waits for them, and re-layouts  1.22 us (1%)
    pallas_call x1, Pallas kernels, body(): pl.pallas_call(kernel, out_shape=jax.ShapeDtypeStruct((2, 16), f32), in_s...  81.2 us

profile of v6, /device:TPU:1, one launch (start us, length us, event | category | flops | bytes accessed | tf_op | source)
XLA Modules:
  0.0 82.5 jit_solution(10882273775013408352)
XLA Ops:
  0.0 0.0 copy-start
  0.0 0.7 copy-done
  0.7 81.2 %shard_map.55 = f32[2,16]{1,0:T(2,128)S(1)} custom-call(bf16[2,64,16,512]{3,2,1,0:T(8,128)(2,1)} %con_hbm.1, bf16[2,64,16,512]{3,2,1,0:T(8,128)(2,1)} %val_hbm.1, bf16[2,2048,512]{2,1,0:T(8,128)(2,1)} %w_hbm.1, bf16[2,16]{1,0:T(2,128)(2,1)S(1)} %copy-done, s32[2,64]{1,0:T(2,128)} %qmap_hbm.1), custom_call_target="tpu_custom_call" | custom-call | tf_op jit(solution)/shard_map/pallas_call | solution.py:305
  81.9 0.6 copy.7
Async XLA Ops:
  0.0 0.7 copy-start

commit v7 on v6

--- a/solution.py
+++ b/solution.py
@@ -10,8 +10,8 @@
 HERE = 15
 GROUPS = ((0, 4), (4, 4), (8, 4), (12, 2), (14, 1), (15, 1))
 Y_OF = (0, 0, 1, 1, 2, 2, 3, 3, 4, 4, 5, 5, 6, 7, 8, 9)
-LO_OF = Y_OF[:15] + (10,)
-PARTNER_OF = ((0, 0),) * 4 + ((1, 1),) * 4 + ((2, 2),) * 4 + ((3, 3),) * 2 + ((4, 4),) + ((5, 6),)
+LO_OF = Y_OF[:14] + (11, 10)
+PARTNER_OF = ((0, 0),) * 4 + ((1, 1),) * 4 + ((2, 2),) * 4 + ((3, 3),) * 2 + ((4, 7),) + ((5, 6),)
 
 
 def group_of(t):
@@ -49,20 +49,18 @@
         pltpu.make_async_copy(w_hbm, w, load_sem.at[1]),
         pltpu.make_async_copy(qmap_hbm, qmap_ref, load_sem.at[2]),
     ]
+    near = [(0, 0, 1, 0, 0), (0, 0, 1, 1, 0), (0, 0, 0, 0, 1), (1, 0, 0, 0, 0), (3, 0, 0, 0, 0), (0, 1, 0, 0, 0), (0, 3, 0, 0, 0)]
     along_x = [(d, 0, 0, 0, 0) for d in (2, 1, 3)]
-    along_z = [(0, d, 0, 0, 0) for d in (2, 1, 3)]
-    along_y = [(0, 0, 0, 1, 0), (0, 0, 1, 0, 0), (0, 0, 1, 1, 0)]
     other_core = [(0, 0, 0, 0, 1)]
-    lines = along_y + along_x + along_z + other_core
     barrier = pltpu.get_barrier_semaphore()
-    for offset in lines:
+    for offset in near:
         pl.semaphore_signal(barrier, inc=1, device_id=dev(*offset), device_id_type=MESH)
     for n in (3, 1, 0):
         loads[n].start()
 
-    def tell(group):
+    def tell(stage, group):
         for offset in group:
-            pl.semaphore_signal(ready, inc=1, device_id=dev(*offset), device_id_type=MESH)
+            pl.semaphore_signal(ready.at[stage], inc=1, device_id=dev(*offset), device_id_type=MESH)
 
     def send(src, dst, ss, rs, to):
         pltpu.make_async_remote_copy(src, dst, ss, rs, device_id=to, device_id_type=MESH).start()
@@ -99,8 +97,8 @@
                         val_all[2 * HERE, q, k] = tile
                     else:
                         buffer[t, q, k] = tile
-    pl.semaphore_wait(barrier, len(lines))
-    tell(along_x + other_core)
+    pl.semaphore_wait(barrier, len(near))
+    tell(0, near)
 
     def val_along_y(t):
         some = pl.ds(t, 3)
@@ -127,7 +125,9 @@
                     else:
                         con_all[0, 0, HERE, 0, q, k] = tile
     loads[2].start()
-    pl.semaphore_wait(ready, 4)
+    pl.semaphore_wait(ready.at[0], len(near))
+    tell(1, along_x + other_core)
+    pl.semaphore_wait(ready.at[1], 4)
     for t in range(15):
         send(qa_all.at[blk], qa_all.at[blk], qa_ss, qa_rs.at[0], dev(*ORDER[t]))
     for block in range(0, 15, 4):
@@ -258,21 +258,20 @@
     others(12, 2)
     terms(12, 2)
     home(12, 2)
-    come(14, 1)
-    own(14, 1)
-    others(14, 1)
-    terms(14, 1)
-    home(14, 1)
-    arrived(con_all.at[0, 1, HERE], y_rs.at[Y_OF[HERE]])
-    forward(HERE, 1, 1)
-    quarter(HERE, 1, 0, 1, True)
-    arrived(con_all.at[0, 0, HERE, 1], y_rs.at[LO_OF[HERE]])
-    forward(HERE, 1, 0)
-    quarter(HERE, 1, 0, 0)
-    arrived(con_all.at[1, 1, HERE], p_rs.at[PARTNER_OF[HERE][1]])
-    quarter(HERE, 1, 1, 1)
-    arrived(con_all.at[1, 0, HERE], p_rs.at[PARTNER_OF[HERE][0]])
-    quarter(HERE, 1, 1, 0)
+    for t in (14, HERE):
+        arrived(con_all.at[0, 0, t, 1], y_rs.at[LO_OF[t]])
+        forward(t, 1, 0)
+        quarter(t, 1, 0, 0, True)
+        arrived(con_all.at[0, 1, t], y_rs.at[Y_OF[t]])
+        forward(t, 1, 1)
+        quarter(t, 1, 0, 1)
+        arrived(con_all.at[1, 0, t], p_rs.at[PARTNER_OF[t][0]])
+        quarter(t, 1, 1, 0)
+        arrived(con_all.at[1, 1, t], p_rs.at[PARTNER_OF[t][1]])
+        quarter(t, 1, 1, 1)
+        if t == 14:
+            terms(14, 1)
+            home(14, 1)
     terms(HERE, 1)
     arrived(gathered, home_rs)
     column = part[HERE] + jnp.sum(gathered[...], axis=0)
@@ -329,7 +328,7 @@
             pltpu.VMEM((15, 2, 2, 128), f32),
             pltpu.VMEM((8, 2, 128), f32),
             pltpu.VMEM((2, 128), f32),
-            pltpu.SemaphoreType.REGULAR, dma((3,)), dma((8,)), dma((11,)), dma((7,)), dma((6,)), dma((5,)), dma((2,)), dma, dma,
+            pltpu.SemaphoreType.REGULAR((2,)), dma((3,)), dma((8,)), dma((12,)), dma((8,)), dma((6,)), dma((5,)), dma((2,)), dma, dma,
             dma, dma, dma, dma, dma, dma, dma, dma,
         ],
         compiler_params=pltpu.CompilerParams(collective_id=0, has_side_effects=True, vmem_limit_bytes=55224 * 1024),

time: 82.6 us -> 82.1 us (level)
  no operation moved by 1% of the time
where the time goes in v7:
time: 82.1 us; the launch traced here: 82 us
  Pallas kernels  80.8 us (98%)
  local copies, waits for them, and re-layouts  1.22 us (1%)
    pallas_call x1, Pallas kernels, body(): pl.pallas_call(kernel, out_shape=jax.ShapeDtypeStruct((2, 16), f32), in_s...  80.8 us

profile of v7, /device:TPU:1, one launch (start us, length us, event | category | flops | bytes accessed | tf_op | source)
XLA Modules:
  0.0 82.0 jit_solution(2514187970064842193)
XLA Ops:
  0.0 0.0 copy-start
  0.0 0.7 copy-done
  0.7 80.8 %shard_map.55 = f32[2,16]{1,0:T(2,128)S(1)} custom-call(bf16[2,64,16,512]{3,2,1,0:T(8,128)(2,1)} %con_hbm.1, bf16[2,64,16,512]{3,2,1,0:T(8,128)(2,1)} %val_hbm.1, bf16[2,2048,512]{2,1,0:T(8,128)(2,1)} %w_hbm.1, bf16[2,16]{1,0:T(2,128)(2,1)S(1)} %copy-done, s32[2,64]{1,0:T(2,128)} %qmap_hbm.1), custom_call_target="tpu_custom_call" | custom-call | tf_op jit(solution)/shard_map/pallas_call | solution.py:304
  81.5 0.6 copy.7
Async XLA Ops:
  0.0 0.7 copy-start

commit v8 on v7

--- a/solution.py
+++ b/solution.py
@@ -277,11 +277,10 @@
     column = part[HERE] + jnp.sum(gathered[...], axis=0)
     fin[ga] = column[0]
     crossing[...] = column[1]
-    for gh in (0, 1):
-        for gc in (0, 1):
-            send(crossing, fin.at[4 + ga], fin_ss, fin_rs, dev(0, 0, 1, gh, gc))
-            if (gh, gc) != (0, 0):
-                send(fin.at[ga], fin.at[ga], fin_ss, fin_rs, dev(0, 0, 0, gh, gc))
+    for gh, gc in ((1, 0), (1, 1), (0, 1)):
+        send(fin.at[ga], fin.at[ga], fin_ss, fin_rs, dev(0, 0, 0, gh, gc))
+    for gh, gc in ((1, 0), (1, 1), (0, 0), (0, 1)):
+        send(crossing, fin.at[4 + ga], fin_ss, fin_rs, dev(0, 0, 1, gh, gc))
     arrived(fin.at[pl.ds(1, 7)], fin_rs)
     out_ref[...] = jnp.sum(fin[...], axis=0)[:, :16] / 64.0
 

time: 82.1 us -> 82.1 us (level)
  no operation moved by 1% of the time
where the time goes in v8:
time: 82.1 us; the launch traced here: 82 us
  Pallas kernels  80.8 us (98%)
  local copies, waits for them, and re-layouts  1.22 us (1%)
    pallas_call x1, Pallas kernels, body(): pl.pallas_call(kernel, out_shape=jax.ShapeDtypeStruct((2, 16), f32), in_s...  80.8 us

profile of v8, /device:TPU:1, one launch (start us, length us, event | category | flops | bytes accessed | tf_op | source)
XLA Modules:
  0.0 82.0 jit_solution(2989491125604319459)
XLA Ops:
  0.0 0.0 copy-start
  0.0 0.7 copy-done
  0.7 80.8 %shard_map.55 = f32[2,16]{1,0:T(2,128)S(1)} custom-call(bf16[2,64,16,512]{3,2,1,0:T(8,128)(2,1)} %con_hbm.1, bf16[2,64,16,512]{3,2,1,0:T(8,128)(2,1)} %val_hbm.1, bf16[2,2048,512]{2,1,0:T(8,128)(2,1)} %w_hbm.1, bf16[2,16]{1,0:T(2,128)(2,1)S(1)} %copy-done, s32[2,64]{1,0:T(2,128)} %qmap_hbm.1), custom_call_target="tpu_custom_call" | custom-call | tf_op jit(solution)/shard_map/pallas_call | solution.py:303
  81.5 0.6 copy.7
Async XLA Ops:
  0.0 0.7 copy-start
